TPU v7x, 32 devices: a whole 2x2x4 slice. The times are simulated.
32 devices in a mesh: rep: 2 (over y), seq: 16 (over z, x, core).
Axes of the slice: x: 2, y: 2, z: 4, core: 2. Of those that a mesh axis runs over, the one named last changes fastest.
Arguments:
- latents: bfloat16 [16, 24576], P(None, ('rep', 'seq')), parts along dimension 1, may hold values from -6 to 6
- layout: int32 [32, 768], P('rep'), parts along dimension 0, may hold values from 0 to 12287, as said below
- assign: int32 [16], P('rep'), parts along dimension 0, may hold values from 0 to 7, as said below
- counts: int32 [16], P('rep'), parts along dimension 0, may hold values from 1 to 3
- latent_cache: bfloat16 [2, 128, 1024], P(None, ('rep', 'seq')), parts along dimension 1, may hold values from -6 to 6
- feature_cache: bfloat16 [2, 128, 64, 384], P(None, ('rep', 'seq')), parts along dimension 1, may hold values from -4 to 4
- first_weight: bfloat16 [3, 3, 3, 16, 384], replicated, may hold values from -0.3125 to 0.3125
- first_bias: float32 [384], replicated, may hold values from -3 to 3
- norm_gain: float32 [384], replicated, may hold values from 0.25 to 1.75
- second_weight: bfloat16 [3, 3, 3, 384, 192], replicated, may hold values from -0.0625 to 0.0625
- second_bias: float32 [192], replicated, may hold values from -3 to 3
Outputs:
- decoded_frames: bfloat16 [3, 256, 128, 192], P(None, ('rep', 'seq')), parts along dimension 1
- latent_cache_next: bfloat16 [2, 128, 1024], P(None, ('rep', 'seq')), parts along dimension 1
- feature_cache_next: bfloat16 [2, 128, 64, 384], P(None, ('rep', 'seq')), parts along dimension 1
There are 2 independent parts, one for each index of `rep`. A program takes and returns all parts, laid end to end along the dimension named above; an argument that names none is the same for every part. Nothing has to cross between parts.
Inputs may be any that keep to these rules, and one draw needn't show every extreme that they name: assign is a permutation of 0 to 7. layout is a permutation of 0 to 12287. Call the cells of request assign[g], rows k * 4 to (k + 1) * 4 - 1, all frames and columns, the tile of seq index (g * 2 + k - 1) mod 16; every row of layout holds exactly 48 cells of every tile.
All inputs are finite; a program needn't handle non-finite values.
Results may differ from a plain program's by a relative error of at most 0.0034.
Values may be sent and summed in bfloat16 or wider, within the bound.
A program may use at most 128 MiB of HBM per device.

v0:
```python
import jax
import jax.numpy as jnp
from jax import lax
from jax.experimental import pallas as pl
from jax.experimental.pallas import tpu as pltpu
from jax.sharding import PartitionSpec as P

LAT_CH = 16
REQS = 8
FMAX = 3
ROWS_DEV = 4
W = 64


def padded_2(array, sides, width):
    for axis, dim in sides:
        devices, length = (lax.axis_size(axis), array.shape[dim])
        up = [(i, (i + 1) % devices) for i in range(devices)]
        down = [(j, i) for i, j in up]
        last = lax.slice_in_dim(array, length - width, length, axis=dim)
        first = lax.slice_in_dim(array, 0, width, axis=dim)
        before = lax.ppermute(last, axis, up)
        after = lax.ppermute(first, axis, down)
        array = jnp.concatenate([before, array, after], axis=dim)
    return array


def tile_numbers(layout, assign, per_group, devices):
    height = ROWS_DEV * per_group
    offset = per_group // 2
    tile_cells = FMAX * ROWS_DEV * W
    column = layout % W
    remain = layout // W
    image_row = remain % height
    remain = remain // height
    frame_index = remain % FMAX
    request = remain // FMAX
    group_ranks = jnp.arange(REQS, dtype=jnp.int32)
    group_index = jnp.sum(jnp.where(assign == request[..., None], group_ranks, 0), axis=-1)
    place = group_index * per_group + image_row // ROWS_DEV
    target = (place - offset + devices) % devices
    within = (frame_index * ROWS_DEV + image_row % ROWS_DEV) * W + column
    return target * tile_cells + within


def keep_rows(values, rim_width, position, height):
    row_index = position * ROWS_DEV - rim_width + jnp.arange(values.shape[1], dtype=jnp.int32)
    inside = (row_index >= 0) & (row_index < height)
    return jnp.where(inside[None, :, None, None], values, jnp.zeros((), values.dtype))


def causal_conv(values, weight, offset):
    result = lax.conv_general_dilated(
        values[None],
        weight,
        (1, 1, 1),
        ((0, 0), (0, 0), (1, 1)),
        dimension_numbers=("NDHWC", "DHWIO", "NDHWC"),
        preferred_element_type=jnp.float32,
    )
    return result[0] + offset


def activate(linear, norm_gain):
    inverse = lax.rsqrt(jnp.mean(linear * linear, axis=-1, keepdims=True) + 1e-06)
    return jax.nn.silu(linear * inverse * norm_gain).astype(jnp.bfloat16)


def decode_kernel(info, cached, fresh, weight, bias, out, carry, shifted, packed):
    frame = pl.program_id(0)
    rows, columns, mid = fresh.shape[1:]
    width = bias.shape[0]
    history = cached.shape[0]

    @pl.when(frame == 0)
    def _prepare():
        def pack(step, _):
            at = pl.multiple_of(step * 16, 16)
            for a in range(3):
                taps = [
                    [weight[a, b, e, pl.ds(at, 16), :].astype(jnp.float32) for e in range(3)]
                    for b in range(3)
                ]
                for py in range(2):
                    if py == 0:
                        lines = (taps[0], [taps[1][e] + taps[2][e] for e in range(3)])
                    else:
                        lines = ([taps[0][e] + taps[1][e] for e in range(3)], taps[2])
                    for px in range(2):
                        for iy, line in enumerate(lines):
                            if px == 0:
                                pair = (line[0], line[1] + line[2])
                            else:
                                pair = (line[0] + line[1], line[2])
                            for ix, value in enumerate(pair):
                                start = ((a * 2 + iy) * 2 + ix) * mid
                                packed[2 * py + px, pl.ds(at, 16), start : start + mid] = value.astype(
                                    jnp.bfloat16
                                )
            return 0

        lax.fori_loop(0, width // 16, pack, 0)
        edge = lax.broadcasted_iota(jnp.int32, (columns, mid), 0)
        for source, count, first in ((cached, history, 0), (fresh, fresh.shape[0], history)):
            def shift(step, _):
                f = step // rows
                r = step % rows
                bad = ((r == 0) & (info[0] == 0)) | ((r == rows - 1) & (info[1] == 0))
                value = jnp.where(bad, 0.0, source[f, r].astype(jnp.float32))
                left = jnp.where(edge == 0, 0.0, pltpu.roll(value, 1, 0))
                right = jnp.where(edge == columns - 1, 0.0, pltpu.roll(value, columns - 1, 0))
                shifted[0, first + f, r] = left.astype(jnp.bfloat16)
                shifted[1, first + f, r] = value.astype(jnp.bfloat16)
                shifted[2, first + f, r] = right.astype(jnp.bfloat16)
                return 0

            lax.fori_loop(0, count * rows, shift, 0)
        for i in range(history):
            carry[i] = shifted[1, info[2] + i, 1 : rows - 1]

    inner = rows - 2
    cells = inner * columns
    live = frame < info[2]
    pair = 2 * columns
    spot = lax.broadcasted_iota(jnp.int32, (2 * pair, 2 * pair), 0)
    goal = spot // pair + 2 * (spot % pair)
    mix = (lax.broadcasted_iota(jnp.int32, (2 * pair, 2 * pair), 1) == goal).astype(jnp.bfloat16)
    for py in range(2):
        halves = []
        for px in range(2):
            parts = []
            for a in range(3):
                for iy in range(2):
                    for ix in range(2):
                        block = shifted[px + ix, frame + a, py + iy : py + iy + inner]
                        parts.append(block.reshape(cells, mid))
            total = lax.dot_general(
                packed[2 * py + px],
                jnp.concatenate(parts, axis=1),
                (((1,), (1,)), ((), ())),
                preferred_element_type=jnp.float32,
            )
            halves.append(jnp.where(live, total + bias[...], 0.0).astype(jnp.bfloat16))
        for i in range(0, inner, 2):
            both = jnp.concatenate(
                [half[:, i * columns : i * columns + pair] for half in halves], axis=1
            )
            mixed = jnp.dot(both, mix, preferred_element_type=jnp.float32).astype(jnp.bfloat16)
            out[0, 2 * i + py] = mixed[:, 0:pair]
            out[0, 2 * i + 2 + py] = mixed[:, pair : 2 * pair]


def decode(info, cached, fresh, weight, bias):
    history, rows, columns, mid = cached.shape
    width = bias.shape[0]
    inner = rows - 2
    frames = fresh.shape[0]
    return pl.pallas_call(
        decode_kernel,
        grid=(frames,),
        in_specs=[
            pl.BlockSpec(memory_space=pltpu.SMEM),
            pl.BlockSpec(cached.shape, lambda t: (0, 0, 0, 0)),
            pl.BlockSpec(fresh.shape, lambda t: (0, 0, 0, 0)),
            pl.BlockSpec(weight.shape, lambda t: (0, 0, 0, 0, 0)),
            pl.BlockSpec((width, 1), lambda t: (0, 0)),
        ],
        out_specs=[
            pl.BlockSpec((1, 2 * inner, width, 2 * columns), lambda t: (t, 0, 0, 0)),
            pl.BlockSpec((history, inner, columns, mid), lambda t: (0, 0, 0, 0)),
        ],
        out_shape=[
            jax.ShapeDtypeStruct((frames, 2 * inner, width, 2 * columns), jnp.bfloat16),
            jax.ShapeDtypeStruct((history, inner, columns, mid), jnp.bfloat16),
        ],
        scratch_shapes=[
            pltpu.VMEM((3, history + frames, rows, columns, mid), jnp.bfloat16),
            pltpu.VMEM((4, width, 12 * mid), jnp.bfloat16),
        ],
        compiler_params=pltpu.CompilerParams(
            dimension_semantics=("arbitrary",), vmem_limit_bytes=56 * 1024 * 1024
        ),
        cost_estimate=pl.CostEstimate(
            flops=2 * frames * inner * columns * 48 * mid * width,
            bytes_accessed=8_000_000,
            transcendentals=0,
        ),
    )(info, cached, fresh, weight, bias[:, None])


def one_hot(values, count, dtype=jnp.bfloat16):
    return (values[..., None] == jnp.arange(count, dtype=jnp.int32)).astype(dtype)


def body(
    latents,
    layout,
    assign,
    counts,
    latent_cache,
    feature_cache,
    first_weight,
    first_bias,
    norm_gain,
    second_weight,
    second_bias,
):
    devices = lax.axis_size("seq")
    myself = lax.axis_index("seq")
    per_group = devices // REQS
    offset = per_group // 2
    height = ROWS_DEV * per_group
    tile_cells = FMAX * ROWS_DEV * W
    per_peer = tile_cells // devices
    numbers = tile_numbers(layout, assign, per_group, devices)
    own_numbers = lax.dynamic_index_in_dim(numbers, myself, 0, keepdims=False)
    send_rank = jnp.sum((own_numbers[None, :] < own_numbers[:, None]).astype(jnp.int32), axis=1)
    outgoing = jnp.dot(latents, one_hot(send_rank, tile_cells)).reshape(LAT_CH, devices, per_peer)
    incoming = lax.all_to_all(outgoing, "seq", split_axis=1, concat_axis=1, tiled=True)
    inside = numbers - myself * tile_cells
    mine = (inside >= 0) & (inside < tile_cells)
    line = jnp.where(mine, inside // W, -1)
    held = jnp.einsum(
        "sph,spl->shl",
        one_hot(line, FMAX * ROWS_DEV),
        one_hot(inside % W, W),
        preferred_element_type=jnp.float32,
    ).reshape(devices, tile_cells)
    cell = jnp.arange(tile_cells, dtype=jnp.int32)
    before = jnp.dot(
        held.astype(jnp.bfloat16),
        (cell[:, None] < cell[None, :]).astype(jnp.bfloat16),
        preferred_element_type=jnp.float32,
    )
    base = jnp.arange(devices, dtype=jnp.float32)[:, None] * per_peer
    slot = jnp.sum(held * (before + base), axis=0).astype(jnp.int32)
    arranged = jnp.dot(
        incoming.reshape(LAT_CH, tile_cells),
        (cell[:, None] == slot[None, :]).astype(jnp.bfloat16),
    )
    window = jnp.transpose(arranged.reshape(LAT_CH, FMAX, ROWS_DEV, W), (1, 2, 3, 0))
    place = (myself + offset) % devices
    position = place % per_group
    request = jnp.take(assign, place // per_group)
    live_frames = jnp.take(counts, request)
    first_input = jnp.concatenate([latent_cache.reshape(2, ROWS_DEV, W, LAT_CH), window], axis=0)
    padded = keep_rows(padded_2(first_input, (("seq", 1),), 2), 2, position, height)
    widened = activate(causal_conv(padded, first_weight, first_bias), norm_gain)
    cached = padded_2(feature_cache, (("seq", 1),), 1)
    info = jnp.stack(
        [
            (position > 0).astype(jnp.int32),
            (position < per_group - 1).astype(jnp.int32),
            live_frames.astype(jnp.int32),
        ]
    )
    decoded_frames, feature_next = decode(
        info, cached, widened, jnp.swapaxes(second_weight, 3, 4), second_bias
    )
    decoded_frames = jnp.swapaxes(decoded_frames, 2, 3)
    latent_next = lax.dynamic_slice_in_dim(first_input, live_frames, 2, 0).reshape(
        2, ROWS_DEV, W * LAT_CH
    )
    return (decoded_frames, latent_next, feature_next)


def solution(mesh):
    return jax.shard_map(
        body,
        mesh=mesh,
        in_specs=(
            P(None, ("rep", "seq")),
            P("rep", None),
            P("rep"),
            P("rep"),
            P(None, ("rep", "seq"), None),
            P(None, ("rep", "seq"), None, None),
            P(),
            P(),
            P(),
            P(),
            P(),
        ),
        out_specs=(
            P(None, ("rep", "seq"), None, None),
            P(None, ("rep", "seq"), None),
            P(None, ("rep", "seq"), None, None),
        ),
        check_vma=False,
    )
```

profile of v0, /device:TPU:0, one launch (start us, length us, event | category | flops | bytes accessed | tf_op | source)
XLA Modules:
  0.0 60.5 jit_solution(2104391879660307371)
XLA Ops:
  0.6 0.0 copy-start
  0.6 0.0 copy-start.6
  0.7 0.9 %add_select_fusion.8 = s32[16,768]{1,0:T(8,128)S(1)} fusion(s32[16,768]{1,0:T(8,128)} %param.12), kind=kLoop, calls=%fused_computation.46 | loop fusion | flops 466944 | bytes 98304 | tf_op jit(solution)/shard_map/jit(floor_divide)/jit(_where)/select_n | solution.py:37
  1.6 0.8 %select_reduce_fusion = s32[16,768]{1,0:T(8,128)S(1)} fusion(s32[16,768]{1,0:T(8,128)S(1)} %add_select_fusion.8, s32[8]{0:T(128)} %param.13), kind=kLoop, calls=%fused_computation.20 | loop fusion | flops 282624 | bytes 98336 | tf_op jit(solution)/shard_map/reduce_sum | solution.py:39
  2.5 1.0 %fusion.20 = (s32[16,768]{1,0:T(8,128)S(1)}, s32[16,768]{1,0:T(8,128)S(1)}) fusion(s32[]{:T(128)S(6)} %mul.63, s32[16,768]{1,0:T(8,128)} %param.12, s32[16,768]{1,0:T(8,128)S(1)} %select_reduce_fusion), kind=kLoop, calls=%fused_computation.64 | loop fusion | flops 1265664 | bytes 196612 | tf_op jit(solution)/shard_map/jit(_where)/select_n | solution.py:222
  3.5 0.4 convert_reduce_fusion
  3.9 1.3 %fusion.8 = bf16[16,768]{1,0:T(8,128)(2,1)S(1)} fusion(bf16[16,768]{1,0:T(8,128)(2,1)} %param.11, s32[768]{0:T(1024)S(1)} %convert_reduce_fusion), kind=kOutput, calls=%fused_computation.16 | convolution fusion | flops 19464192 | bytes 52224 | tf_op jit(solution)/shard_map/dot_general | solution.py:218
  5.2 0.1 reshape.125
  5.3 0.0 copy-start.7
  5.3 0.0 copy-start.2
  5.4 0.7 %reshape.192 = bf16[16,2,384]{2,1,0:T(2,128)(2,1)} reshape(bf16[16,16,48]{2,1,0:T(8,128)(2,1)S(1)} %bitcast.36) | data formatting | bytes 49152
  6.1 7.4 %all-to-all-start = ((bf16[16,2,384]{2,1,0:T(2,128)(2,1)}), bf16[16,2,384]{2,1,0:T(2,128)(2,1)S(1)}, u32[]{:S(2)}, u32[]{:S(2)}) async-start(bf16[16,2,384]{2,1,0:T(2,128)(2,1)} %reshape.192), calls=%async_computation | async-start | bytes 49152 | tf_op jit(solution)/shard_map/all_to_all | solution.py:219
  13.5 0.0 copy-start.5
  13.5 1.0 %fusion.36 = (bf16[2,1,64,384]{3,2,1,0:T(8,128)(2,1)S(1)}, bf16[2,1,64,384]{3,2,1,0:T(8,128)(2,1)S(1)}) fusion(bf16[2,4,64,384]{3,2,1,0:T(8,128)(2,1)} %param.16), kind=kLoop, calls=%fused_computation.91 | loop fusion | bytes 393216 | tf_op jit(solution)/shard_map/slice | solution.py:20
  14.5 0.5 collective-permute-start
  14.9 4.0 %collective-permute-start.1 = (bf16[2,1,64,384]{3,2,1,0:T(8,128)(2,1)S(1)}, bf16[2,1,64,384]{3,2,1,0:T(8,128)(2,1)S(1)}, u32[]{:S(2)}, u32[]{:S(2)}) collective-permute-start(bf16[2,1,64,384]{3,2,1,0:T(8,128)(2,1)S(1)} %get-tuple-element.32), channel_id=1, source_target_pairs={{1,0},{2,1},{3,2},{4,3},{5,4},{6,5},{7,6},{8,7},{9,8},{10,9},{11,1... | collective-permute-start | bytes 294920 | tf_op jit(solution)/shard_map/ppermute | solution.py:23
  19.1 0.0 copy-done.6
  19.1 0.6 dynamic-slice.4
  20.3 0.7 %fusion = f32[16,12,64]{2,1,0:T(8,128)S(1)} fusion(s32[16,768]{1,0:T(8,128)S(1)} %add_select_fusion, s32[16,768]{1,0:T(8,128)S(1)} %get-tuple-element.29), kind=kOutput, calls=%fused_computation.1 | convolution fusion | flops 19808256 | bytes 147456 | tf_op jit(solution)/shard_map/sph,spl->shl/dot_general | solution.py:223
  21.0 0.1 reshape.124
  21.1 0.2 fusion.7
  21.4 0.4 iota_compare_fusion.4
  21.8 0.0 copy-done.7
  21.8 0.6 dynamic-slice.5
  23.0 0.6 pad_add_fusion.info
  23.6 0.0 copy-done.2
  23.6 0.1 reshape.123
  23.7 0.1 copy.27
  23.8 0.0 copy-done.5
  23.8 0.8 %copy.29.bias = f32[192,1]{1,0:T(8,128)} copy(f32[192,1]{0,1:T(1,128)S(1)} %bitcast.40) | data formatting | bytes 1536 | tf_op jit(solution)/shard_map/broadcast_in_dim | solution.py:188
  24.6 0.0 all-to-all-done
  24.6 0.1 reshape.193
  24.8 0.1 reshape.189
  24.9 0.6 fusion.32
  25.5 0.5 collective-permute-start.3
  26.0 0.1 collective-permute-start.2
  26.1 0.1 copy.30
  26.2 0.8 %reshape.127 = bf16[2,4,1024]{2,1,0:T(4,128)(2,1)} reshape(bf16[2,4,64,16]{3,2,1,0:T(8,128)(2,1)S(1)} %copy.30) | data formatting | bytes 32768 | tf_op jit(solution)/shard_map/reshape | solution.py:261
  27.0 0.6 %collective-permute-done.3 = bf16[5,2,64,16]{2,3,1,0:T(8,128)(2,1)S(1)} collective-permute-done((bf16[5,2,64,16]{2,3,1,0:T(8,128)(2,1)S(1)}, bf16[5,2,64,16]{2,3,1,0:T(8,128)(2,1)S(1)}, u32[]{:S(2)}, u32[]{:S(2)}) %collective-permute-start.3) | collective-permute-done | bytes 20512 | tf_op jit(solution)/shard_map/ppermute | solution.py:23
  27.7 4.4 %collective-permute-done.2 = bf16[5,2,64,16]{2,3,1,0:T(8,128)(2,1)S(1)} collective-permute-done((bf16[5,2,64,16]{2,3,1,0:T(8,128)(2,1)S(1)}, bf16[5,2,64,16]{2,3,1,0:T(8,128)(2,1)S(1)}, u32[]{:S(2)}, u32[]{:S(2)}) %collective-permute-start.2) | collective-permute-done | bytes 20512 | tf_op jit(solution)/shard_map/ppermute | solution.py:22
  32.1 0.1 maximum_select_fusion
  32.2 0.9 %copy.28 = bf16[1,5,8,64,16]{4,0,3,2,1:T(2,128)(2,1)S(1)} copy(bf16[1,5,8,64,16]{3,4,2,1,0:T(8,128)(2,1)S(1)} %maximum_select_fusion) | data formatting | bytes 163840 | tf_op jit(solution)/shard_map/jit(_where)/select_n | solution.py:49
  33.1 0.0 copy-done
  33.1 0.0 copy-start.3
  33.1 8.1 %fusion.37 = f32[1,3,6,64,384]{4,0,3,2,1:T(1,128)S(1)} fusion(bf16[1,5,8,64,16]{4,0,3,2,1:T(2,128)(2,1)S(1)} %copy.28, bf16[3,3,3,16,384]{4,3,2,1,0:T(8,128)(2,1)S(1)} %copy-done), kind=kOutput, calls=%fused_computation.93 | convolution fusion | flops 378224640 | bytes 2183168 | tf_op jit(solution)/shard_map/conv_general_dilated | solution.py:53
  41.1 0.0 copy-done.3
  41.1 0.0 copy-start.4
  41.2 0.2 multiply_reduce_fusion
  41.4 0.0 copy-start.1
  41.4 0.4 copy-done.4
  41.8 1.5 %multiply_convert_fusion.fresh = bf16[3,6,64,384]{3,2,1,0:T(8,128)(2,1)} fusion(f32[1,3,6,64,384]{4,0,3,2,1:T(1,128)S(1)} %fusion.37, f32[384]{0:T(512)S(1)} %copy-done.4, f32[3,6,64]{2,1,0:T(8,128)S(1)} %add_rsqrt_fusion, f32[384]{0:T(512)S(1)} %copy-done.3), kind=kLoop, calls=%fused_computation.9 | loop fusion | flops 3538944 | bytes 2661888 | tf_op jit(solution)/shard_map/convert_element_type | solution.py:66
  43.3 0.0 collective-permute-done
  43.3 0.0 collective-permute-done.1
  43.3 0.0 copy-done.1
  43.3 0.9 %pad_maximum_fusion.cached = bf16[2,6,64,384]{3,2,1,0:T(8,128)(2,1)} fusion(bf16[2,1,64,384]{3,2,1,0:T(8,128)(2,1)S(1)} %collective-permute-done.1, bf16[2,4,64,384]{3,2,1,0:T(8,128)(2,1)S(1)} %copy-done.1, bf16[2,1,64,384]{3,2,1,0:T(8,128)(2,1)S(1)} %collective-permute-done), kind=kLoop, calls=%fused_computation.18 | loop fusion | flops 589824 | bytes 1179648 | tf_op jit(solution)/shard_map/concatenate | solution.py:24
  44.3 16.3 %shard_map.130 = (bf16[3,8,192,128]{3,2,1,0:T(8,128)(2,1)}, bf16[2,4,64,384]{3,2,1,0:T(8,128)(2,1)}) custom-call(s32[3]{0:T(128)} %pad_add_fusion.info, bf16[2,6,64,384]{3,2,1,0:T(8,128)(2,1)} %pad_maximum_fusion.cached, bf16[3,6,64,384]{3,2,1,0:T(8,128)(2,1)} %multiply_convert_fusion.fresh, bf16[3,3,3,192,384]{4,3,2,1,0:T(8,128)(2,1)} %bitcast.41, ...), custom_call_target="tpu_custom_call" | custom-call | flops 5435817984 | bytes 8000000 | tf_op jit(solution)/shard_map/pallas_call | solution.py:158
  (11 shorter events, 0.2 us)
Async XLA Ops:
  0.6 32.4 %copy-start = (bf16[3,3,3,16,384]{4,3,2,1,0:T(8,128)(2,1)S(1)}, bf16[3,3,3,16,384]{4,3,2,1,0:T(8,128)(2,1)}, u32[]{:S(2)}) copy-start(bf16[3,3,3,16,384]{4,3,2,1,0:T(8,128)(2,1)} %param.17) | copy-start | bytes 995332
  0.6 18.4 %copy-start.6 = (s32[8]{0:T(128)S(1)}, s32[8]{0:T(128)}, u32[]{:S(2)}) copy-start(s32[8]{0:T(128)} %param.13) | copy-start | bytes 100
  5.3 16.5 %copy-start.7 = (s32[8]{0:T(128)S(1)}, s32[8]{0:T(128)}, u32[]{:S(2)}) copy-start(s32[8]{0:T(128)} %param.14) | copy-start | bytes 100
  5.3 18.2 %copy-start.2 = (bf16[2,4,1024]{2,1,0:T(4,128)(2,1)S(1)}, bf16[2,4,1024]{2,1,0:T(4,128)(2,1)}, u32[]{:S(2)}) copy-start(bf16[2,4,1024]{2,1,0:T(4,128)(2,1)} %param.15) | copy-start | bytes 49156
  6.1 18.5 %all-to-all-start = ((bf16[16,2,384]{2,1,0:T(2,128)(2,1)}), bf16[16,2,384]{2,1,0:T(2,128)(2,1)S(1)}, u32[]{:S(2)}, u32[]{:S(2)}) async-start(bf16[16,2,384]{2,1,0:T(2,128)(2,1)} %reshape.192), calls=%async_computation | async-start | bytes 49152 | tf_op jit(solution)/shard_map/all_to_all | solution.py:219
  13.5 10.3 %copy-start.5 = (f32[192]{0:T(256)S(1)}, f32[192]{0:T(256)}, u32[]{:S(2)}) copy-start(f32[192]{0:T(256)} %param.21) | copy-start | bytes 2308
  14.5 28.9 %collective-permute-start = (bf16[2,1,64,384]{3,2,1,0:T(8,128)(2,1)S(1)}, bf16[2,1,64,384]{3,2,1,0:T(8,128)(2,1)S(1)}, u32[]{:S(2)}, u32[]{:S(2)}) collective-permute-start(bf16[2,1,64,384]{3,2,1,0:T(8,128)(2,1)S(1)} %get-tuple-element.31), channel_id=1, source_target_pairs={{0,1},{1,2},{2,3},{3,4},{4,5},{5,6},{6,7},{7,8},{8,9},{9,10},{10,1... | collective-permute-start | bytes 294920 | tf_op jit(solution)/shard_map/ppermute | solution.py:22
  14.9 28.4 %collective-permute-start.1 = (bf16[2,1,64,384]{3,2,1,0:T(8,128)(2,1)S(1)}, bf16[2,1,64,384]{3,2,1,0:T(8,128)(2,1)S(1)}, u32[]{:S(2)}, u32[]{:S(2)}) collective-permute-start(bf16[2,1,64,384]{3,2,1,0:T(8,128)(2,1)S(1)} %get-tuple-element.32), channel_id=1, source_target_pairs={{1,0},{2,1},{3,2},{4,3},{5,4},{6,5},{7,6},{8,7},{9,8},{10,9},{11,1... | collective-permute-start | bytes 294920 | tf_op jit(solution)/shard_map/ppermute | solution.py:23
  25.5 2.1 %collective-permute-start.3 = (bf16[5,2,64,16]{2,3,1,0:T(8,128)(2,1)S(1)}, bf16[5,2,64,16]{2,3,1,0:T(8,128)(2,1)S(1)}, u32[]{:S(2)}, u32[]{:S(2)}) collective-permute-start(bf16[5,2,64,16]{2,3,1,0:T(8,128)(2,1)S(1)} %get-tuple-element.34), channel_id=1, source_target_pairs={{1,0},{2,1},{3,2},{4,3},{5,4},{6,5},{7,6},{8,7},{9,8},{10,9},{11,1... | collective-permute-start | bytes 61448 | tf_op jit(solution)/shard_map/ppermute | solution.py:23
  26.0 6.1 %collective-permute-start.2 = (bf16[5,2,64,16]{2,3,1,0:T(8,128)(2,1)S(1)}, bf16[5,2,64,16]{2,3,1,0:T(8,128)(2,1)S(1)}, u32[]{:S(2)}, u32[]{:S(2)}) collective-permute-start(bf16[5,2,64,16]{2,3,1,0:T(8,128)(2,1)S(1)} %get-tuple-element.33), channel_id=1, source_target_pairs={{0,1},{1,2},{2,3},{3,4},{4,5},{5,6},{6,7},{7,8},{8,9},{9,10},{10,1... | collective-permute-start | bytes 61448 | tf_op jit(solution)/shard_map/ppermute | solution.py:22
  33.1 8.1 %copy-start.3 = (f32[384]{0:T(512)S(1)}, f32[384]{0:T(512)}, u32[]{:S(2)}) copy-start(f32[384]{0:T(512)} %param.18) | copy-start | bytes 4612
  41.1 0.7 %copy-start.4 = (f32[384]{0:T(512)S(1)}, f32[384]{0:T(512)}, u32[]{:S(2)}) copy-start(f32[384]{0:T(512)} %param.19) | copy-start | bytes 4612
  41.4 1.9 %copy-start.1 = (bf16[2,4,64,384]{3,2,1,0:T(8,128)(2,1)S(1)}, bf16[2,4,64,384]{3,2,1,0:T(8,128)(2,1)}, u32[]{:S(2)}) copy-start(bf16[2,4,64,384]{3,2,1,0:T(8,128)(2,1)} %param.16) | copy-start | bytes 1179652
where the time goes:
time: 60.9 us; the launch traced here: 60.5 us
  Pallas kernels  16.3 us (27%)
  starting transfers between devices  12.4 us (20%)
  matrix products  10.8 us (18%)
  other arithmetic  7.04 us (12%)
  local copies, waits for them, and re-layouts  6.63 us (11%)
  waiting for transfers between devices  5.08 us (8%)
  between operations  2.26 us (4%)
    pallas_call x1, Pallas kernels, decode(): pl.pallas_call(decode_kernel, grid=(frames,), in_specs=[pl.BlockSpec(memo...  16.3 us
    conv_general_dilated x1, matrix products, causal_conv(): lax.conv_general_dilated(values[None], weight, (1, 1, 1), ((0, 0), (0, 0)...  8.07 us
    all_to_all x1, starting transfers between devices, body(): lax.all_to_all(outgoing, 'seq', split_axis=1, concat_axis=1, tiled=True)  7.39 us
    ppermute x2, starting transfers between devices, padded_2(): after = lax.ppermute(first, axis, down)  4.5 us
    ppermute x2, waiting for transfers between devices, padded_2(): before = lax.ppermute(last, axis, up)  4.45 us
    convert_element_type x1, other arithmetic, activate(): return jax.nn.silu(linear * inverse * norm_gain).astype(jnp.bfloat16)  1.5 us
    unnamed x18, local copies, waits for them, and re-layouts  1.3 us
    dot_general x1, matrix products, body(): jnp.dot(latents, one_hot(send_rank, tile_cells))  1.27 us
  transfers between devices with their start and end apart: 5, of which 2 were waited for; matrix products, arithmetic and copies ran while one was open for 29% of the time, Pallas kernels for 0%

commit v1 on v0

v1 whole, which is shorter than its diff:
```python
import functools

import jax
import jax.numpy as jnp
from jax import lax
from jax.experimental import pallas as pl
from jax.experimental.pallas import tpu as pltpu
from jax.sharding import PartitionSpec as P

LAT_CH = 16
REQS = 8
FMAX = 3
ROWS_DEV = 4
W = 64
F32 = jnp.float32
BF16 = jnp.bfloat16


def lane_index(shape):
    return lax.broadcasted_iota(jnp.int32, shape, len(shape) - 1)


def column_of(row, lanes):
    return jnp.transpose(jnp.broadcast_to(row, (lanes, row.shape[1])))


def sublane_index(shape):
    return lax.broadcasted_iota(jnp.int32, shape, len(shape) - 2)


def trips(count, step, carry=None):
    body = lambda i, c: step(i) or 0
    lax.fori_loop(0, count, body, 0, unroll=True if count <= 16 else 1)


def ranks_in(mask, before):
    rows, slots = mask.shape
    blocks = slots // 128
    stacked = jnp.concatenate([mask[:, i * 128 : i * 128 + 128] for i in range(blocks)], axis=0)
    counted = jnp.dot(stacked.astype(BF16), before, preferred_element_type=F32)
    base = jnp.zeros((rows, 128), F32)
    ranks = []
    for i in range(blocks):
        block = counted[i * rows : (i + 1) * rows]
        ranks.append(block[:, 0:128] + base)
        base = base + block[:, 128:256]
    return jnp.where(mask > 0.0, jnp.concatenate(ranks, axis=1), -1.0)


def place_of(device, devices, per_group):
    place = lax.rem(device + per_group // 2, devices)
    return place // per_group, lax.rem(place, per_group)


def exchange_kernel(
    devices,
    assign,
    latents,
    layout,
    latent_cache,
    feature_cache,
    first,
    halo,
    outgoing,
    incoming,
    past,
    edges,
    row_line,
    row_column,
    row_rank,
    line_mask,
    column_hot,
    send_sem,
    recv_sem,
    edge_send,
    edge_recv,
    halo_send,
    halo_recv,
):
    me = lax.axis_index("seq")
    per_group = devices // REQS
    slots = layout.shape[1]
    history, inner, wide = latent_cache.shape
    height = inner * per_group
    span = min(3, per_group)
    starts = per_group - span + 1
    used = -(-span * (slots // devices) // 16) * 16
    lines = FMAX * (inner + 4)
    group, position = place_of(me, devices, per_group)
    above = lax.rem(me + devices - 1, devices)
    below = lax.rem(me + 1, devices)

    barrier = pltpu.get_barrier_semaphore()

    def greet(i):
        pl.semaphore_signal(barrier, inc=1, device_id={"seq": lax.rem(me + 1 + i, devices)})

    trips(devices - 1, greet)

    for f in range(history):
        stacked = []
        for r in range(inner):
            row = jnp.broadcast_to(latent_cache[f, r : r + 1, :].astype(F32), (LAT_CH, wide))
            mine = sublane_index(row.shape) == lane_index(row.shape) % LAT_CH
            stacked.append(jnp.where(mine, row, 0.0).astype(BF16))
        pick = sublane_index((wide, 128)) // LAT_CH == lane_index((wide, 128)) % W
        turned = jnp.dot(
            jnp.concatenate(stacked, axis=0), pick.astype(BF16), preferred_element_type=F32
        ).astype(BF16)
        for r in range(0, inner, 2):
            low = turned[r * LAT_CH : (r + 1) * LAT_CH]
            high = turned[(r + 1) * LAT_CH : (r + 2) * LAT_CH]
            left = lane_index(low.shape) < W
            past[f, r // 2] = jnp.where(left, low, high)

    square = (128, 256)
    earlier = (sublane_index(square) < lane_index(square)) | (lane_index(square) >= 128)
    before = earlier.astype(BF16)
    mine = layout[pl.ds(me, 1), :]
    remain = mine // W
    row = lax.rem(remain, height)
    step = remain // height
    windows = REQS * starts
    window = sublane_index((windows, slots))
    request = jnp.zeros((windows, slots), jnp.int32)
    for g in range(REQS):
        request = jnp.where(window // starts == g, assign[g], request)
    low = lax.rem(window, starts) * inner
    member = (step >= request * FMAX) & (step < request * FMAX + FMAX)
    member = member & (row >= low) & (row < low + span * inner)
    rank = ranks_in(jnp.where(member, 1.0, 0.0), before)
    row_rank[0:windows] = rank

    def chosen(i):
        ranked = row_rank[pl.ds(i, 1), :]
        hot = sublane_index((used, slots)).astype(F32) == ranked
        hot = jnp.where(hot, 1.0, 0.0).astype(BF16)
        if used < 128:
            hot = jnp.concatenate([hot, jnp.zeros((128 - used, slots), BF16)], axis=0)
        return hot

    def collect(i):
        hot = jnp.concatenate([chosen(2 * i), chosen(2 * i + 1)], axis=0)
        moved = lax.dot_general(
            latents[...], hot, (((1,), (1,)), ((), ())), preferred_element_type=F32
        ).astype(BF16)
        outgoing[2 * i] = moved[:, 0:128]
        outgoing[2 * i + 1] = moved[:, 128:256]

    trips(windows // 2, collect)

    pl.semaphore_wait(barrier, devices - 1)

    def window_of(device):
        g, k = place_of(device, devices, per_group)
        return g * starts + jnp.clip(k - 1, 0, starts - 1)

    def copy_to(i):
        peer = lax.rem(me + 1 + i, devices)
        return pltpu.make_async_remote_copy(
            src_ref=outgoing.at[window_of(peer)],
            dst_ref=incoming.at[me],
            send_sem=send_sem.at[peer],
            recv_sem=recv_sem.at[me],
            device_id={"seq": peer},
        )

    trips(devices - 1, lambda i: copy_to(i).start())

    def edge_copies(side):
        peer = (above, below)[side]
        copies = []
        for f in range(history):
            copies.append(
                pltpu.make_async_remote_copy(
                    src_ref=past.at[f, 0 if side == 0 else inner // 2 - 1],
                    dst_ref=edges.at[1 - side, f],
                    send_sem=edge_send.at[side, f],
                    recv_sem=edge_recv.at[1 - side, f],
                    device_id={"seq": peer},
                )
            )
            copies.append(
                pltpu.make_async_remote_copy(
                    src_ref=feature_cache.at[f, 0 if side == 0 else inner - 1],
                    dst_ref=halo.at[1 - side, f],
                    send_sem=halo_send.at[side, f],
                    recv_sem=halo_recv.at[1 - side, f],
                    device_id={"seq": peer},
                )
            )
        return copies

    has = (position > 0, position < per_group - 1)
    for side in range(2):

        @pl.when(has[side])
        def _start():
            for copy in edge_copies(side):
                copy.start()

    incoming[me] = outgoing[window_of(me)]

    number = layout[...]
    remain = number // W
    row = lax.rem(remain, height)
    step = remain // height - assign[group] * FMAX
    first_tile = jnp.clip(position - 1, 0, starts - 1)
    member = (step >= 0) & (step < FMAX)
    member = member & (row >= first_tile * inner) & (row < (first_tile + span) * inner)
    rank = ranks_in(jnp.where(member, 1.0, 0.0), before)
    local = row - (position * inner - 2)
    line = jnp.where((local >= 0) & (local < inner + 4), step * (inner + 4) + local + 1, 0)
    row_rank[0:devices] = rank
    row_line[...] = line.astype(F32)
    row_column[...] = lax.rem(number, W).astype(F32)

    def locate(i):
        ranked = row_rank[pl.ds(i, 1), :]
        hot = sublane_index((128, slots)).astype(F32) == ranked
        hot = jnp.where(hot, 1.0, 0.0).astype(BF16)
        shape = (16, slots)
        what = jnp.where(
            sublane_index(shape) == 0, row_line[pl.ds(i, 1), :], row_column[pl.ds(i, 1), :]
        ).astype(BF16)
        found = lax.dot_general(what, hot, (((1,), (1,)), ((), ())), preferred_element_type=F32)
        level = sublane_index((lines * LAT_CH, 128)) // LAT_CH + 1
        line_mask[i] = jnp.where(level.astype(F32) == found[0:1], 1.0, 0.0).astype(BF16)
        column = jnp.transpose(jnp.broadcast_to(found[1:2], (128, 128)))
        same = column == (lane_index((128, 128)) % W).astype(F32)
        column_hot[pl.ds(pl.multiple_of(i * 128, 128), 128)] = jnp.where(same, 1.0, 0.0).astype(BF16)

    trips(devices, locate)

    for side in range(2):

        @pl.when(jnp.logical_not(has[side]))
        def _clear():
            edges[side] = jnp.zeros(edges.shape[1:], BF16)

        @pl.when(has[side])
        def _arrive():
            for copy in edge_copies(1 - side):
                copy.wait_recv()

    def arrive(i):
        peer = lax.rem(me + 1 + i, devices)
        pltpu.make_async_remote_copy(
            src_ref=outgoing.at[0],
            dst_ref=incoming.at[peer],
            send_sem=send_sem.at[peer],
            recv_sem=recv_sem.at[peer],
            device_id={"seq": peer},
        ).wait_recv()

    trips(devices - 1, arrive)

    def place(i, total):
        pieces = []
        for half in range(2):
            got = incoming[2 * i + half]
            pieces.append(jnp.concatenate([got] * lines, axis=0) * line_mask[2 * i + half])
        hot = column_hot[pl.ds(pl.multiple_of(i * 256, 256), 256)]
        return total + jnp.dot(jnp.concatenate(pieces, axis=1), hot, preferred_element_type=F32)

    pairs = devices // 2
    placed = lax.fori_loop(
        0,
        pairs,
        place,
        jnp.zeros((lines * LAT_CH, 128), F32),
        unroll=True if pairs <= 16 else 1,
    )
    left = lane_index((LAT_CH, 128)) < W
    block = (inner + 4) * W
    for i in range(lines // 2):
        low = placed[2 * i * LAT_CH : (2 * i + 1) * LAT_CH]
        high = placed[(2 * i + 1) * LAT_CH : (2 * i + 2) * LAT_CH]
        start = history * block + i * 128
        first[:, start : start + 128] = jnp.where(left, low, high).astype(BF16)
    for f in range(history):
        first[:, f * block : f * block + 128] = edges[0, f]
        for r in range(inner // 2):
            start = f * block + 128 + r * 128
            first[:, start : start + 128] = past[f, r]
        first[:, f * block + block - 128 : f * block + block] = edges[1, f]

    trips(devices - 1, lambda i: copy_to(i).wait_send())
    for side in range(2):

        @pl.when(has[side])
        def _sent():
            for copy in edge_copies(side):
                copy.wait_send()


def exchange(assign, latents, layout, latent_cache, feature_cache):
    devices, slots = layout.shape
    history, inner, _, mid = feature_cache.shape
    per_group = devices // REQS
    windows = REQS * (per_group - min(3, per_group) + 1)
    lines = FMAX * (inner + 4)
    vmem = pl.BlockSpec(memory_space=pltpu.VMEM)
    return pl.pallas_call(
        functools.partial(exchange_kernel, devices),
        in_specs=[pl.BlockSpec(memory_space=pltpu.SMEM), vmem, vmem, vmem, pl.BlockSpec(memory_space=pl.ANY)],
        out_specs=[vmem, pl.BlockSpec(memory_space=pl.ANY)],
        out_shape=[
            jax.ShapeDtypeStruct((LAT_CH, (history + FMAX) * (inner + 4) * W), BF16),
            jax.ShapeDtypeStruct((2, history, W, mid), BF16),
        ],
        scratch_shapes=[
            pltpu.VMEM((windows, LAT_CH, 128), BF16),
            pltpu.VMEM((devices, LAT_CH, 128), BF16),
            pltpu.VMEM((history, inner // 2, LAT_CH, 128), BF16),
            pltpu.VMEM((2, history, LAT_CH, 128), BF16),
            pltpu.VMEM((devices, slots), F32),
            pltpu.VMEM((devices, slots), F32),
            pltpu.VMEM((max(devices, windows), slots), F32),
            pltpu.VMEM((devices, lines * LAT_CH, 128), BF16),
            pltpu.VMEM((devices * 128, 128), BF16),
            pltpu.SemaphoreType.DMA((devices,)),
            pltpu.SemaphoreType.DMA((devices,)),
            pltpu.SemaphoreType.DMA((2, history)),
            pltpu.SemaphoreType.DMA((2, history)),
            pltpu.SemaphoreType.DMA((2, history)),
            pltpu.SemaphoreType.DMA((2, history)),
        ],
        compiler_params=pltpu.CompilerParams(
            collective_id=0, has_side_effects=True, vmem_limit_bytes=48 * 1024 * 1024
        ),
    )(assign, latents, layout, latent_cache, feature_cache)


def decode_kernel(
    assign, counts, first, cached, halo, w1, b1, gain, w2, b2, out, carry, latent_next, feat, packed, pre, columns
):
    frame = pl.program_id(0)
    history, inner, _, mid = cached.shape
    width = b2.shape[0]
    rows = inner + 2
    cells = inner * W
    devices = lax.axis_size("seq")
    per_group = devices // REQS
    group, position = place_of(lax.axis_index("seq"), devices, per_group)
    has = (position > 0, position < per_group - 1)
    count = counts[assign[group]]
    span = rows * W
    frames = FMAX

    col = lane_index((16, span)) % W
    keep = ((col != 0).astype(BF16), None, (col != W - 1).astype(BF16))

    def spread(f, value, ch, count):
        value = value.astype(BF16)
        for e in range(3):
            whole = value if e == 1 else pltpu.roll(value, (1, 0, span - 1)[e], 1) * keep[e]
            feat[e, f, pl.ds(ch, count), 0:span] = whole
            below = pltpu.roll(value, span - W + 1 - e, 1)[:, 0:cells]
            feat[e, f, pl.ds(ch, count), span : span + cells] = below if e == 1 else below * keep[e][:, 0:cells]

    @pl.when(frame == 0)
    def _prepare():
        def pack(step, _):
            at = pl.multiple_of(step * 16, 16)
            for a in range(3):
                taps = [
                    [w2[a, b, e, pl.ds(at, 16), :].astype(F32) for e in range(3)] for b in range(3)
                ]
                for py in range(2):
                    if py == 0:
                        lines = (taps[0], [taps[1][e] + taps[2][e] for e in range(3)])
                    else:
                        lines = ([taps[0][e] + taps[1][e] for e in range(3)], taps[2])
                    for px in range(2):
                        for iy, line in enumerate(lines):
                            if px == 0:
                                pair = (line[0], line[1] + line[2])
                            else:
                                pair = (line[0] + line[1], line[2])
                            for ix, value in enumerate(pair):
                                start = ((a * 2 + iy) * 2 + ix) * mid
                                packed[2 * py + px, pl.ds(at, 16), start : start + mid] = value.astype(BF16)
            return 0

        lax.fori_loop(0, width // 16, pack, 0)

        columns[0, 0:mid] = column_of(b1[...].reshape(1, mid), 128)
        columns[1, 0:mid] = column_of(gain[...].reshape(1, mid), 128)
        columns[2, 0:width] = column_of(b2[...].reshape(1, width), 128)

        for f in range(history):
            sides = [jnp.where(has[i], halo[i, f], jnp.zeros((), BF16)) for i in range(2)]
            tall = jnp.concatenate([sides[0], cached[f].reshape(cells, mid), sides[1]], axis=0)
            pre[...] = jnp.transpose(tall.astype(F32))

            def turn(step, _):
                at = pl.multiple_of(step * 16, 16)
                spread(f, pre[pl.ds(at, 16), :], at, 16)
                return 0

            lax.fori_loop(0, mid // 16, turn, 0, unroll=True)

        value = first[...].astype(F32)
        total = value.shape[1]
        col = lane_index(value.shape) % W
        left = jnp.where(col == 0, 0.0, pltpu.roll(value, 1, 1))
        right = jnp.where(col == W - 1, 0.0, pltpu.roll(value, total - 1, 1))
        shifts = [v.astype(BF16) for v in (left, value, right)]
        later = [pltpu.roll(v, total - W, 1).astype(BF16) for v in (left, value, right)]
        block = (rows + 2) * W
        row = lane_index((16, span)) // W
        outside = ((row == 0) & jnp.logical_not(has[0])) | ((row == rows - 1) & jnp.logical_not(has[1]))
        for t in range(frames):
            patch = []
            for a in range(3):
                for b in range(3):
                    source, begin = (later, 0) if b == 1 else (shifts, b * W)
                    begin += (t + a) * block
                    for e in range(3):
                        patch.append(source[e][:, begin : begin + span])
            pre[...] = lax.dot_general(
                w1[...].reshape(27 * LAT_CH, mid),
                jnp.concatenate(patch, axis=0),
                (((0,), (0,)), ((), ())),
                preferred_element_type=F32,
            )

            def square(step, acc):
                at = pl.multiple_of(step * 16, 16)
                bias = columns[0, pl.ds(at, 16)]
                x = pre[pl.ds(at, 16), :] + jnp.concatenate([bias] * (span // 128), axis=1)
                pre[pl.ds(at, 16), :] = x
                return acc + x * x

            squares = lax.fori_loop(0, mid // 16, square, jnp.zeros((16, span), F32), unroll=True)
            inverse = lax.rsqrt(jnp.sum(squares, axis=0, keepdims=True) / mid + 1e-06)

            def finish(step, _):
                at = pl.multiple_of(step * 16, 16)
                scale = columns[1, pl.ds(at, 16)]
                x = pre[pl.ds(at, 16), :] * inverse * jnp.concatenate([scale] * (span // 128), axis=1)
                x = x / (1.0 + jnp.exp(-x))
                spread(history + t, jnp.where(outside, 0.0, x), at, 16)
                return 0

            lax.fori_loop(0, mid // 16, finish, 0, unroll=True)

        live = count
        for i in range(history):
            carry[i] = jnp.transpose(feat[1, live + i, :, span : span + cells].astype(F32)).astype(
                BF16
            ).reshape(inner, W, mid)
        parts = []
        for i in range(history):
            start = pl.multiple_of((live + i) * block + 2 * W, 128)
            own = first[:, pl.ds(start, cells)].astype(F32)
            for r in range(inner):
                parts.append(own[:, r * W : (r + 1) * W])
        stacked = jnp.concatenate(parts, axis=0).astype(BF16)
        pick = lax.broadcasted_iota(jnp.int32, (W, W * LAT_CH), 0) == lane_index((W, W * LAT_CH)) // LAT_CH
        wide = jnp.dot(stacked, pick.astype(BF16), preferred_element_type=F32)
        wide = wide.reshape(history * inner, LAT_CH, W * LAT_CH)
        mine = lax.broadcasted_iota(jnp.int32, wide.shape, 1) == lane_index(wide.shape) % LAT_CH
        latent_next[...] = (
            jnp.sum(jnp.where(mine, wide, 0.0), axis=1).astype(BF16).reshape(history, inner, W * LAT_CH)
        )

    live = frame < count
    pair = 2 * W
    spot = lax.broadcasted_iota(jnp.int32, (2 * pair, 2 * pair), 0)
    goal = spot // pair + 2 * (spot % pair)
    mix = (lane_index((2 * pair, 2 * pair)) == goal).astype(BF16)
    bias = jnp.concatenate([columns[2, 0:width]] * (cells // 128), axis=1)
    for py in range(2):
        halves = []
        for px in range(2):
            parts = []
            for a in range(3):
                for iy in range(2):
                    begin = (0, span, 2 * W)[py + iy]
                    for ix in range(2):
                        parts.append(feat[px + ix, frame + a, :, begin : begin + cells])
            total = jnp.dot(
                packed[2 * py + px], jnp.concatenate(parts, axis=0), preferred_element_type=F32
            )
            halves.append(jnp.where(live, total + bias, 0.0).astype(BF16))
        for i in range(0, inner, 2):
            both = jnp.concatenate([half[:, i * W : i * W + pair] for half in halves], axis=1)
            mixed = jnp.dot(both, mix, preferred_element_type=F32).astype(BF16)
            out[0, 2 * i + py] = mixed[:, 0:pair]
            out[0, 2 * i + 2 + py] = mixed[:, pair : 2 * pair]


def decode(assign, counts, first, cached, halo, w1, b1, gain, w2, b2):
    history, inner, _, mid = cached.shape
    width = b2.shape[0]
    rows = inner + 2
    frames = FMAX
    whole = lambda array: pl.BlockSpec(array.shape, lambda t: (0,) * array.ndim)
    return pl.pallas_call(
        decode_kernel,
        grid=(frames,),
        in_specs=[pl.BlockSpec(memory_space=pltpu.SMEM)] * 2
        + [whole(array) for array in (first, cached, halo, w1, b1, gain, w2, b2)],
        out_specs=[
            pl.BlockSpec((1, 2 * inner, width, 2 * W), lambda t: (t, 0, 0, 0)),
            pl.BlockSpec((history, inner, W, mid), lambda t: (0, 0, 0, 0)),
            pl.BlockSpec((history, inner, W * LAT_CH), lambda t: (0, 0, 0)),
        ],
        out_shape=[
            jax.ShapeDtypeStruct((frames, 2 * inner, width, 2 * W), BF16),
            jax.ShapeDtypeStruct((history, inner, W, mid), BF16),
            jax.ShapeDtypeStruct((history, inner, W * LAT_CH), BF16),
        ],
        scratch_shapes=[
            pltpu.VMEM((3, history + frames, mid, (rows + inner) * W), BF16),
            pltpu.VMEM((4, width, 12 * mid), BF16),
            pltpu.VMEM((mid, rows * W), F32),
            pltpu.VMEM((3, mid, 128), F32),
        ],
        compiler_params=pltpu.CompilerParams(
            dimension_semantics=("arbitrary",), vmem_limit_bytes=56 * 1024 * 1024
        ),
        cost_estimate=pl.CostEstimate(
            flops=2 * frames * inner * W * 48 * mid * width,
            bytes_accessed=8_000_000,
            transcendentals=0,
        ),
    )(assign, counts, first, cached, halo, w1, b1, gain, w2, b2)


def body(
    latents,
    layout,
    assign,
    counts,
    latent_cache,
    feature_cache,
    first_weight,
    first_bias,
    norm_gain,
    second_weight,
    second_bias,
):
    first, halo = exchange(assign, latents, layout, latent_cache, feature_cache)
    decoded_frames, feature_next, latent_next = decode(
        assign,
        counts,
        first,
        feature_cache,
        halo,
        first_weight,
        first_bias,
        norm_gain,
        jnp.swapaxes(second_weight, 3, 4),
        second_bias,
    )
    return (jnp.swapaxes(decoded_frames, 2, 3), latent_next, feature_next)


def solution(mesh):
    return jax.shard_map(
        body,
        mesh=mesh,
        in_specs=(
            P(None, ("rep", "seq")),
            P("rep", None),
            P("rep"),
            P("rep"),
            P(None, ("rep", "seq"), None),
            P(None, ("rep", "seq"), None, None),
            P(),
            P(),
            P(),
            P(),
            P(),
        ),
        out_specs=(
            P(None, ("rep", "seq"), None, None),
            P(None, ("rep", "seq"), None),
            P(None, ("rep", "seq"), None, None),
        ),
        check_vma=False,
    )
```

time: 60.9 us -> 33.4 us (0.55)
  starting transfers between devices: 12.4 us -> 0 us
  matrix products: 10.8 us -> 0 us
  Pallas kernels: 16.3 us -> 27 us
  other arithmetic: 7.04 us -> 0 us
  waiting for transfers between devices: 5.08 us -> 0 us
  between operations: 2.26 us -> 0.66 us
  local copies, waits for them, and re-layouts: 6.63 us -> 5.18 us
    pallas_call x0 -> x1, Pallas kernels: none -> 11.4 us  [exchange(): pl.pallas_call(functools.partial(exchange_kernel, devices), in_specs=[pl....]
    conv_general_dilated x1 -> x0, matrix products: 8.07 us -> none  [causal_conv(): lax.conv_general_dilated(values[None], weight, (1, 1, 1), ((0, 0), (0, 0)...]
    all_to_all x1 -> x0, starting transfers between devices: 7.39 us -> none  [body(): lax.all_to_all(outgoing, 'seq', split_axis=1, concat_axis=1, tiled=True)]
    ppermute x4 -> x0, waiting for transfers between devices: 5.08 us -> none  [the longest x2 4.45 us: padded_2(): before = lax.ppermute(last, axis, up)]
    ppermute x4 -> x0, starting transfers between devices: 5.06 us -> none  [the longest x2 4.5 us: padded_2(): after = lax.ppermute(first, axis, down)]
    unnamed x18 -> x14, local copies, waits for them, and re-layouts: 1.3 us -> 5.18 us
    dot_general x4 -> x0, matrix products: 2.75 us -> none  [the longest x1 1.27 us: body(): jnp.dot(latents, one_hot(send_rank, tile_cells))]
    select_n x4 -> x0, other arithmetic: 2.08 us -> none  [the longest x1 1.03 us: body(): line = jnp.where(mine, inside // W, -1)]
  transfers between devices with their start and end apart: 5 -> 0, of which waited for: 2 -> 0; matrix products, arithmetic and copies ran while one was open for 29% -> 0% of each run, Pallas kernels for 0% -> 0%
where the time goes in v1:
time: 33.4 us; the launch traced here: 32.8 us
  Pallas kernels  27 us (81%)
  local copies, waits for them, and re-layouts  5.18 us (16%)
  between operations  0.66 us (2%)
    pallas_call x1, Pallas kernels, decode(): pl.pallas_call(decode_kernel, grid=(frames,), in_specs=[pl.BlockSpec(memo...  15.5 us
    pallas_call x1, Pallas kernels, exchange(): pl.pallas_call(functools.partial(exchange_kernel, devices), in_specs=[pl....  11.4 us
    unnamed x14, local copies, waits for them, and re-layouts  5.18 us

profile of v1, /device:TPU:0, one launch (start us, length us, event | category | flops | bytes accessed | tf_op | source)
XLA Modules:
  0.0 32.8 jit_solution(14915141526611177959)
XLA Ops:
  0.6 0.0 copy-start
  0.6 1.0 %copy-done = bf16[2,4,64,384]{3,2,1,0:T(8,128)(2,1)S(1)} copy-done((bf16[2,4,64,384]{3,2,1,0:T(8,128)(2,1)S(1)}, bf16[2,4,64,384]{3,2,1,0:T(8,128)(2,1)}, u32[]{:S(2)}) %copy-start) | copy-done | bytes 393240
  1.6 0.0 copy-start.1
  1.6 0.8 %copy-done.1 = s32[16,768]{1,0:T(8,128)S(1)} copy-done((s32[16,768]{1,0:T(8,128)S(1)}, s32[16,768]{1,0:T(8,128)}, u32[]{:S(2)}) %copy-start.1) | copy-done | bytes 49176
  2.4 0.0 copy-start.2
  2.4 0.7 %copy-done.2 = bf16[16,768]{1,0:T(8,128)(2,1)S(1)} copy-done((bf16[16,768]{1,0:T(8,128)(2,1)S(1)}, bf16[16,768]{1,0:T(8,128)(2,1)}, u32[]{:S(2)}) %copy-start.2) | copy-done | bytes 24600
  3.2 0.0 copy-start.3
  3.2 0.7 %copy-done.3 = bf16[2,4,1024]{2,1,0:T(4,128)(2,1)S(1)} copy-done((bf16[2,4,1024]{2,1,0:T(4,128)(2,1)S(1)}, bf16[2,4,1024]{2,1,0:T(4,128)(2,1)}, u32[]{:S(2)}) %copy-start.3) | copy-done | bytes 16408
  3.9 0.0 copy-start.4
  3.9 0.7 %copy-done.4 = s32[8]{0:T(128)S(1)} copy-done((s32[8]{0:T(128)S(1)}, s32[8]{0:T(128)}, u32[]{:S(2)}) %copy-start.4) | copy-done | bytes 56
  4.5 11.4 %shard_map.130 = (bf16[16,2560]{1,0:T(8,128)(2,1)S(1)}, bf16[2,2,64,384]{3,2,1,0:T(8,128)(2,1)S(1)}) custom-call(s32[8]{0:T(128)S(1)} %copy-done.4, bf16[16,768]{1,0:T(8,128)(2,1)S(1)} %copy-done.2, s32[16,768]{1,0:T(8,128)S(1)} %copy-done.1, bf16[2,4,1024]{2,1,0:T(4,128)(2,1)S(1)} %copy-done.3, bf16[2,4,64,384]{3,2,1,0:T(8,128)(2,1)S(1)} %copy-done), custom_call_target="tpu_custom_call" | custom-call | tf_op jit(solution)/shard_map/pallas_call | solution.py:304
  16.0 0.0 copy-start.5
  16.0 0.7 %copy-done.5 = bf16[2,2,64,384]{3,2,1,0:T(8,128)(2,1)} copy-done((bf16[2,2,64,384]{3,2,1,0:T(8,128)(2,1)}, bf16[2,2,64,384]{3,2,1,0:T(8,128)(2,1)S(1)}, u32[]{:S(2)}) %copy-start.5) | copy-done | bytes 196632
  16.6 0.0 copy-start.6
  16.6 0.6 %copy-done.6 = bf16[16,2560]{1,0:T(8,128)(2,1)} copy-done((bf16[16,2560]{1,0:T(8,128)(2,1)}, bf16[16,2560]{1,0:T(8,128)(2,1)S(1)}, u32[]{:S(2)}) %copy-start.6) | copy-done | bytes 81944
  17.3 15.5 %shard_map.131 = (bf16[3,8,192,128]{3,2,1,0:T(8,128)(2,1)}, bf16[2,4,64,384]{3,2,1,0:T(8,128)(2,1)}, bf16[2,4,1024]{2,1,0:T(4,128)(2,1)}) custom-call(s32[8]{0:T(128)} %assign.3, s32[8]{0:T(128)} %counts.1, bf16[16,2560]{1,0:T(8,128)(2,1)} %copy-done.6, bf16[2,4,64,384]{3,2,1,0:T(8,128)(2,1)} %cached.1, bf16[2,2,64,384]{3,2,1,0:T(8,128)(2,1)} %copy-done.5, ...), custom_call_target="tpu_custom_call" | custom-call | flops 5435817984 | bytes 8000000 | tf_op jit(solution)/shard_map/pallas_call | solution.py:501
Async XLA Ops:
  0.6 1.0 %copy-start = (bf16[2,4,64,384]{3,2,1,0:T(8,128)(2,1)S(1)}, bf16[2,4,64,384]{3,2,1,0:T(8,128)(2,1)}, u32[]{:S(2)}) copy-start(bf16[2,4,64,384]{3,2,1,0:T(8,128)(2,1)} %cached.1) | copy-start | bytes 1179652
  1.6 0.8 %copy-start.1 = (s32[16,768]{1,0:T(8,128)S(1)}, s32[16,768]{1,0:T(8,128)}, u32[]{:S(2)}) copy-start(s32[16,768]{1,0:T(8,128)} %layout.1) | copy-start | bytes 147460
  2.4 0.7 %copy-start.2 = (bf16[16,768]{1,0:T(8,128)(2,1)S(1)}, bf16[16,768]{1,0:T(8,128)(2,1)}, u32[]{:S(2)}) copy-start(bf16[16,768]{1,0:T(8,128)(2,1)} %latents.1) | copy-start | bytes 73732
  3.2 0.7 %copy-start.3 = (bf16[2,4,1024]{2,1,0:T(4,128)(2,1)S(1)}, bf16[2,4,1024]{2,1,0:T(4,128)(2,1)}, u32[]{:S(2)}) copy-start(bf16[2,4,1024]{2,1,0:T(4,128)(2,1)} %latent_cache.1) | copy-start | bytes 49156
  3.9 0.7 %copy-start.4 = (s32[8]{0:T(128)S(1)}, s32[8]{0:T(128)}, u32[]{:S(2)}) copy-start(s32[8]{0:T(128)} %assign.3) | copy-start | bytes 100
  16.0 0.7 %copy-start.5 = (bf16[2,2,64,384]{3,2,1,0:T(8,128)(2,1)}, bf16[2,2,64,384]{3,2,1,0:T(8,128)(2,1)S(1)}, u32[]{:S(2)}) copy-start(bf16[2,2,64,384]{3,2,1,0:T(8,128)(2,1)S(1)} %get-tuple-element.9.halo) | copy-start | bytes 589828
  16.6 0.6 %copy-start.6 = (bf16[16,2560]{1,0:T(8,128)(2,1)}, bf16[16,2560]{1,0:T(8,128)(2,1)S(1)}, u32[]{:S(2)}) copy-start(bf16[16,2560]{1,0:T(8,128)(2,1)S(1)} %get-tuple-element.8.first) | copy-start | bytes 245764

commit v2 on v1

v2 whole, which is shorter than its diff:
```python
import functools

import jax
import jax.numpy as jnp
from jax import lax
from jax.experimental import pallas as pl
from jax.experimental.pallas import tpu as pltpu
from jax.sharding import PartitionSpec as P

LAT_CH = 16
REQS = 8
FMAX = 3
ROWS_DEV = 4
W = 64
F32 = jnp.float32
BF16 = jnp.bfloat16


def lane_index(shape):
    return lax.broadcasted_iota(jnp.int32, shape, len(shape) - 1)


def in_hbm(array):
    return pltpu.with_memory_space_constraint(array, pltpu.HBM)


def column_of(row, lanes):
    return jnp.transpose(jnp.broadcast_to(row, (lanes, row.shape[1])))


def sublane_index(shape):
    return lax.broadcasted_iota(jnp.int32, shape, len(shape) - 2)


def trips(count, step, carry=None):
    body = lambda i, c: step(i) or 0
    lax.fori_loop(0, count, body, 0, unroll=True if count <= 16 else 1)


def ranks_in(mask, before):
    rows, slots = mask.shape
    blocks = slots // 128
    stacked = jnp.concatenate([mask[:, i * 128 : i * 128 + 128] for i in range(blocks)], axis=0)
    counted = jnp.dot(stacked.astype(BF16), before, preferred_element_type=F32)
    base = jnp.zeros((rows, 128), F32)
    ranks = []
    for i in range(blocks):
        block = counted[i * rows : (i + 1) * rows]
        ranks.append(block[:, 0:128] + base)
        base = base + block[:, 128:256]
    return jnp.where(mask > 0.0, jnp.concatenate(ranks, axis=1), -1.0)


def place_of(device, devices, per_group):
    place = lax.rem(device + per_group // 2, devices)
    return place // per_group, lax.rem(place, per_group)


def section_kernel(
    devices,
    assign_hbm,
    latents_hbm,
    layout_hbm,
    latent_cache_hbm,
    feature_cache_hbm,
    w1_hbm,
    b1_hbm,
    gain_hbm,
    w2_hbm,
    b2_hbm,
    halves,
    center,
    first,
    assign,
    latents,
    layout,
    latent_cache,
    feature_cache,
    w1,
    b1,
    gain,
    w2,
    b2,
    halo,
    outgoing,
    incoming,
    past,
    edges,
    row_line,
    row_column,
    row_rank,
    line_mask,
    column_hot,
    feat,
    packed,
    partial,
    pre,
    columns,
    load_sem,
    send_sem,
    recv_sem,
    edge_send,
    edge_recv,
    halo_send,
    halo_recv,
):
    me = lax.axis_index("seq")
    per_group = devices // REQS
    slots = layout.shape[1]
    history, inner, wide = latent_cache.shape
    height = inner * per_group
    span = min(3, per_group)
    starts = per_group - span + 1
    used = -(-span * (slots // devices) // 16) * 16
    lines = FMAX * (inner + 4)
    group, position = place_of(me, devices, per_group)
    above = lax.rem(me + devices - 1, devices)
    below = lax.rem(me + 1, devices)

    loads = [
        pltpu.make_async_copy(source, target, load_sem.at[i])
        for i, (source, target) in enumerate(
            (
                (assign_hbm, assign),
                (layout_hbm, layout),
                (latents_hbm, latents),
                (latent_cache_hbm, latent_cache),
                (feature_cache_hbm, feature_cache),
                (w2_hbm, w2),
                (w1_hbm, w1),
                (b1_hbm, b1),
                (gain_hbm, gain),
                (b2_hbm, b2),
            )
        )
    ]
    for load in loads:
        load.start()

    barrier = pltpu.get_barrier_semaphore()

    def greet(i):
        pl.semaphore_signal(barrier, inc=1, device_id={"seq": lax.rem(me + 1 + i, devices)})

    trips(devices - 1, greet)

    for load in loads[0:4]:
        load.wait()

    for f in range(history):
        stacked = []
        for r in range(inner):
            row = jnp.broadcast_to(latent_cache[f, r : r + 1, :].astype(F32), (LAT_CH, wide))
            mine = sublane_index(row.shape) == lane_index(row.shape) % LAT_CH
            stacked.append(jnp.where(mine, row, 0.0).astype(BF16))
        pick = sublane_index((wide, 128)) // LAT_CH == lane_index((wide, 128)) % W
        turned = jnp.dot(
            jnp.concatenate(stacked, axis=0), pick.astype(BF16), preferred_element_type=F32
        ).astype(BF16)
        for r in range(0, inner, 2):
            low = turned[r * LAT_CH : (r + 1) * LAT_CH]
            high = turned[(r + 1) * LAT_CH : (r + 2) * LAT_CH]
            left = lane_index(low.shape) < W
            past[f, r // 2] = jnp.where(left, low, high)

    square = (128, 256)
    earlier = (sublane_index(square) < lane_index(square)) | (lane_index(square) >= 128)
    before = earlier.astype(BF16)
    mine = layout[pl.ds(me, 1), :]
    remain = mine // W
    row = lax.rem(remain, height)
    step = remain // height
    windows = REQS * starts
    window = sublane_index((windows, slots))
    request = jnp.zeros((windows, slots), jnp.int32)
    for g in range(REQS):
        request = jnp.where(window // starts == g, assign[g], request)
    low = lax.rem(window, starts) * inner
    member = (step >= request * FMAX) & (step < request * FMAX + FMAX)
    member = member & (row >= low) & (row < low + span * inner)
    rank = ranks_in(jnp.where(member, 1.0, 0.0), before)
    row_rank[0:windows] = rank

    def chosen(i):
        ranked = row_rank[pl.ds(i, 1), :]
        hot = sublane_index((used, slots)).astype(F32) == ranked
        hot = jnp.where(hot, 1.0, 0.0).astype(BF16)
        if used < 128:
            hot = jnp.concatenate([hot, jnp.zeros((128 - used, slots), BF16)], axis=0)
        return hot

    def collect(i):
        hot = jnp.concatenate([chosen(2 * i), chosen(2 * i + 1)], axis=0)
        moved = lax.dot_general(
            latents[...], hot, (((1,), (1,)), ((), ())), preferred_element_type=F32
        ).astype(BF16)
        outgoing[2 * i] = moved[:, 0:128]
        outgoing[2 * i + 1] = moved[:, 128:256]

    trips(windows // 2, collect)

    pl.semaphore_wait(barrier, devices - 1)

    def window_of(device):
        g, k = place_of(device, devices, per_group)
        return g * starts + jnp.clip(k - 1, 0, starts - 1)

    def copy_to(i):
        peer = lax.rem(me + 1 + i, devices)
        return pltpu.make_async_remote_copy(
            src_ref=outgoing.at[window_of(peer)],
            dst_ref=incoming.at[me],
            send_sem=send_sem.at[peer],
            recv_sem=recv_sem.at[me],
            device_id={"seq": peer},
        )

    trips(devices - 1, lambda i: copy_to(i).start())
    for load in loads[4:]:
        load.wait()

    def edge_copies(side):
        peer = (above, below)[side]
        copies = []
        for f in range(history):
            copies.append(
                pltpu.make_async_remote_copy(
                    src_ref=past.at[f, 0 if side == 0 else inner // 2 - 1],
                    dst_ref=edges.at[1 - side, f],
                    send_sem=edge_send.at[side, f],
                    recv_sem=edge_recv.at[1 - side, f],
                    device_id={"seq": peer},
                )
            )
            copies.append(
                pltpu.make_async_remote_copy(
                    src_ref=feature_cache.at[f, 0 if side == 0 else inner - 1],
                    dst_ref=halo.at[1 - side, f],
                    send_sem=halo_send.at[side, f],
                    recv_sem=halo_recv.at[1 - side, f],
                    device_id={"seq": peer},
                )
            )
        return copies

    has = (position > 0, position < per_group - 1)
    for side in range(2):

        @pl.when(has[side])
        def _start():
            for copy in edge_copies(side):
                copy.start()

    incoming[me] = outgoing[window_of(me)]

    number = layout[...]
    remain = number // W
    row = lax.rem(remain, height)
    step = remain // height - assign[group] * FMAX
    first_tile = jnp.clip(position - 1, 0, starts - 1)
    member = (step >= 0) & (step < FMAX)
    member = member & (row >= first_tile * inner) & (row < (first_tile + span) * inner)
    rank = ranks_in(jnp.where(member, 1.0, 0.0), before)
    local = row - (position * inner - 2)
    line = jnp.where((local >= 0) & (local < inner + 4), step * (inner + 4) + local + 1, 0)
    row_rank[0:devices] = rank
    row_line[...] = line.astype(F32)
    row_column[...] = lax.rem(number, W).astype(F32)

    def locate(i):
        ranked = row_rank[pl.ds(i, 1), :]
        hot = sublane_index((128, slots)).astype(F32) == ranked
        hot = jnp.where(hot, 1.0, 0.0).astype(BF16)
        shape = (16, slots)
        what = jnp.where(
            sublane_index(shape) == 0, row_line[pl.ds(i, 1), :], row_column[pl.ds(i, 1), :]
        ).astype(BF16)
        found = lax.dot_general(what, hot, (((1,), (1,)), ((), ())), preferred_element_type=F32)
        level = sublane_index((lines * LAT_CH, 128)) // LAT_CH + 1
        line_mask[i] = jnp.where(level.astype(F32) == found[0:1], 1.0, 0.0).astype(BF16)
        column = jnp.transpose(jnp.broadcast_to(found[1:2], (128, 128)))
        same = column == (lane_index((128, 128)) % W).astype(F32)
        column_hot[pl.ds(pl.multiple_of(i * 128, 128), 128)] = jnp.where(same, 1.0, 0.0).astype(BF16)

    trips(devices, locate)

    mid = feature_cache.shape[3]
    width = b2.shape[0]
    cells = inner * W
    high_rows = inner + 2
    stretch = high_rows * W
    col = lane_index((16, stretch)) % W
    keep = ((col != 0).astype(BF16), None, (col != W - 1).astype(BF16))

    shifted = (feat.at[0], center, feat.at[1])

    def spread(f, value, ch):
        value = value.astype(BF16)
        for e in range(3):
            whole = value if e == 1 else pltpu.roll(value, (1, 0, stretch - 1)[e], 1) * keep[e]
            shifted[e][f, ch : ch + 16, 0:stretch] = whole
            below = pltpu.roll(value, stretch - W + 1 - e, 1)[:, 0:cells]
            below = below if e == 1 else below * keep[e][:, 0:cells]
            shifted[e][f, ch : ch + 16, stretch : stretch + cells] = below

    def pack(i):
        at = pl.multiple_of(i * 16, 16)
        for a in range(3):
            taps = [[w2[a, b, e, pl.ds(at, 16), :].astype(F32) for e in range(3)] for b in range(3)]
            for py in range(2):
                if py == 0:
                    pair_of_lines = (taps[0], [taps[1][e] + taps[2][e] for e in range(3)])
                else:
                    pair_of_lines = ([taps[0][e] + taps[1][e] for e in range(3)], taps[2])
                for px in range(2):
                    for iy, taken in enumerate(pair_of_lines):
                        if px == 0:
                            pair = (taken[0], taken[1] + taken[2])
                        else:
                            pair = (taken[0] + taken[1], taken[2])
                        for ix, value in enumerate(pair):
                            start = ((a * 2 + iy) * 2 + ix) * mid
                            packed[2 * py + px, pl.ds(at, 16), start : start + mid] = value.astype(BF16)

    lax.fori_loop(0, width // 16, lambda i, c: pack(i) or 0, 0)
    columns[0, 0:mid] = column_of(b1[...].reshape(1, mid), 128)
    columns[1, 0:mid] = column_of(gain[...].reshape(1, mid), 128)
    columns[2, 0:width] = column_of(b2[...].reshape(1, width), 128)

    for side in range(2):

        @pl.when(jnp.logical_not(has[side]))
        def _clear():
            edges[side] = jnp.zeros(edges.shape[1:], BF16)

        @pl.when(has[side])
        def _arrive():
            for copy in edge_copies(1 - side):
                copy.wait_recv()

    for f in range(history):
        sides = [jnp.where(has[i], halo[i, f], jnp.zeros((), BF16)) for i in range(2)]
        tall = jnp.concatenate([sides[0], feature_cache[f].reshape(cells, mid), sides[1]], axis=0)
        pre[...] = jnp.transpose(tall.astype(F32))
        for ch in range(0, mid, 16):
            spread(f, pre[ch : ch + 16, :], ch)

    def convolve(t, phase, taken):
        py, px = phase // 2, phase % 2
        parts = []
        for a in taken:
            for iy in range(2):
                begin = (0, stretch, 2 * W)[py + iy]
                for ix in range(2):
                    parts.append(shifted[px + ix][t + a, :, begin : begin + cells])
        begin, end = taken[0] * 4 * mid, (taken[-1] + 1) * 4 * mid
        return jnp.dot(
            packed[phase, :, begin:end], jnp.concatenate(parts, axis=0), preferred_element_type=F32
        )

    for t in range(history):
        for phase in range(4):
            partial[t, phase] = convolve(t, phase, range(history - t))

    def arrive(i):
        peer = lax.rem(me + 1 + i, devices)
        pltpu.make_async_remote_copy(
            src_ref=outgoing.at[0],
            dst_ref=incoming.at[peer],
            send_sem=send_sem.at[peer],
            recv_sem=recv_sem.at[peer],
            device_id={"seq": peer},
        ).wait_recv()

    trips(devices - 1, arrive)

    def place(i, total):
        pieces = []
        for half in range(2):
            got = incoming[2 * i + half]
            pieces.append(jnp.concatenate([got] * lines, axis=0) * line_mask[2 * i + half])
        hot = column_hot[pl.ds(pl.multiple_of(i * 256, 256), 256)]
        return total + jnp.dot(jnp.concatenate(pieces, axis=1), hot, preferred_element_type=F32)

    pairs = devices // 2
    placed = lax.fori_loop(
        0,
        pairs,
        place,
        jnp.zeros((lines * LAT_CH, 128), F32),
        unroll=True if pairs <= 16 else 1,
    )
    left = lane_index((LAT_CH, 128)) < W
    block = (inner + 4) * W
    for i in range(lines // 2):
        low = placed[2 * i * LAT_CH : (2 * i + 1) * LAT_CH]
        high = placed[(2 * i + 1) * LAT_CH : (2 * i + 2) * LAT_CH]
        start = history * block + i * 128
        first[:, start : start + 128] = jnp.where(left, low, high).astype(BF16)
    for f in range(history):
        first[:, f * block : f * block + 128] = edges[0, f]
        for r in range(inner // 2):
            start = f * block + 128 + r * 128
            first[:, start : start + 128] = past[f, r]
        first[:, f * block + block - 128 : f * block + block] = edges[1, f]

    value = first[...].astype(F32)
    total = value.shape[1]
    col = lane_index(value.shape) % W
    left = jnp.where(col == 0, 0.0, pltpu.roll(value, 1, 1))
    right = jnp.where(col == W - 1, 0.0, pltpu.roll(value, total - 1, 1))
    shifts = [v.astype(BF16) for v in (left, value, right)]
    later = [pltpu.roll(v, total - W, 1).astype(BF16) for v in (left, value, right)]
    row = lane_index((16, stretch)) // W
    outside = ((row == 0) & jnp.logical_not(has[0])) | ((row == high_rows - 1) & jnp.logical_not(has[1]))
    bias = jnp.concatenate([columns[2, 0:width]] * (cells // 128), axis=1)
    for t in range(FMAX):
        patch = []
        for a in range(3):
            for b in range(3):
                source, begin = (later, 0) if b == 1 else (shifts, b * W)
                begin += (t + a) * block
                for e in range(3):
                    patch.append(source[e][:, begin : begin + stretch])
        pre[...] = lax.dot_general(
            w1[...].reshape(27 * LAT_CH, mid),
            jnp.concatenate(patch, axis=0),
            (((0,), (0,)), ((), ())),
            preferred_element_type=F32,
        )
        squares = jnp.zeros((16, stretch), F32)
        for ch in range(0, mid, 16):
            x = pre[ch : ch + 16, :]
            x = x + jnp.concatenate([columns[0, ch : ch + 16]] * (stretch // 128), axis=1)
            pre[ch : ch + 16, :] = x
            squares = squares + x * x
        inverse = lax.rsqrt(jnp.sum(squares, axis=0, keepdims=True) / mid + 1e-06)
        for ch in range(0, mid, 16):
            scale = jnp.concatenate([columns[1, ch : ch + 16]] * (stretch // 128), axis=1)
            x = pre[ch : ch + 16, :] * inverse * scale
            x = x / (1.0 + jnp.exp(-x))
            spread(history + t, jnp.where(outside, 0.0, x), ch)
        for phase in range(4):
            result = convolve(t, phase, range(max(history - t, 0), 3))
            if t < history:
                result = result + partial[t, phase]
            halves[t, phase] = (result + bias).astype(BF16)

    trips(devices - 1, lambda i: copy_to(i).wait_send())
    for side in range(2):

        @pl.when(has[side])
        def _sent():
            for copy in edge_copies(side):
                copy.wait_send()


def finish_kernel(
    assign_hbm,
    counts_hbm,
    halves,
    center,
    first,
    out,
    carry,
    latent_next,
    assign,
    counts,
    out_buf,
    carry_buf,
    latent_buf,
    load_sem,
    sems,
):
    loads = [
        pltpu.make_async_copy(assign_hbm, assign, load_sem.at[0]),
        pltpu.make_async_copy(counts_hbm, counts, load_sem.at[1]),
    ]
    for load in loads:
        load.start()
    frames, _, width, cells = halves.shape
    history, inner, _, mid = carry.shape
    devices = lax.axis_size("seq")
    group, _ = place_of(lax.axis_index("seq"), devices, devices // REQS)
    pair = 2 * W
    stores = []

    def store(source, target):
        copy = pltpu.make_async_copy(source, target, sems.at[len(stores)])
        copy.start()
        stores.append(copy)

    spot = sublane_index((2 * pair, 2 * pair))
    goal = spot // pair + 2 * (spot % pair)
    mix = (lane_index((2 * pair, 2 * pair)) == goal).astype(BF16)
    for t in range(frames):
        if t == 1:
            for load in loads:
                load.wait()
            count = counts[assign[group]]
        for i in range(0, inner, 2):
            for py in range(2):
                both = jnp.concatenate(
                    [halves[t, 2 * py + px, :, i * W : i * W + pair] for px in range(2)], axis=1
                )
                mixed = jnp.dot(both, mix, preferred_element_type=F32).astype(BF16)
                if t > 0:
                    mixed = jnp.where(t < count, mixed, jnp.zeros((), BF16))
                out_buf[t, 2 * i + py] = mixed[:, 0:pair]
                out_buf[t, 2 * i + 2 + py] = mixed[:, pair : 2 * pair]
        store(out_buf.at[t], out.at[t])
    for i in range(history):
        turned = jnp.transpose(center[count + i, :, (inner + 2) * W :].astype(F32)).astype(BF16)
        carry_buf[i] = turned.reshape(inner, W, mid)
    store(carry_buf, carry)
    parts = []
    for i in range(history):
        start = pl.multiple_of((count + i) * (inner + 4) * W + 2 * W, 128)
        own = first[:, pl.ds(start, cells)].astype(F32)
        for r in range(inner):
            parts.append(own[:, r * W : (r + 1) * W])
    stacked = jnp.concatenate(parts, axis=0).astype(BF16)
    shape = (W, W * LAT_CH)
    pick = sublane_index(shape) == lane_index(shape) // LAT_CH
    wide = jnp.dot(stacked, pick.astype(BF16), preferred_element_type=F32)
    wide = wide.reshape(history * inner, LAT_CH, W * LAT_CH)
    mine = sublane_index(wide.shape) == lane_index(wide.shape) % LAT_CH
    latent_buf[...] = (
        jnp.sum(jnp.where(mine, wide, 0.0), axis=1).astype(BF16).reshape(history, inner, W * LAT_CH)
    )
    store(latent_buf, latent_next)
    for copy in stores:
        copy.wait()


def section(assign, counts, latents, layout, latent_cache, feature_cache, w1, b1, gain, w2, b2):
    devices, slots = layout.shape
    history, inner, _, mid = feature_cache.shape
    width = b2.shape[0]
    per_group = devices // REQS
    windows = REQS * (per_group - min(3, per_group) + 1)
    lines = FMAX * (inner + 4)
    cells = inner * W
    stretch = (inner + 2) * W
    vmem = pl.BlockSpec(memory_space=pltpu.VMEM)
    hbm = pl.BlockSpec(memory_space=pltpu.HBM)
    inputs = (assign, latents, layout, latent_cache, feature_cache, w1, b1, gain, w2, b2)
    halves, center, first = pl.pallas_call(
        functools.partial(section_kernel, devices),
        in_specs=[hbm] * len(inputs),
        out_specs=[vmem] * 3,
        out_shape=[
            jax.ShapeDtypeStruct((FMAX, 4, width, cells), BF16),
            jax.ShapeDtypeStruct((history + FMAX, mid, stretch + cells), BF16),
            jax.ShapeDtypeStruct((LAT_CH, (history + FMAX) * (inner + 4) * W), BF16),
        ],
        scratch_shapes=[(pltpu.SMEM if i < 1 else pltpu.VMEM)(x.shape, x.dtype) for i, x in enumerate(inputs)]
        + [
            pltpu.VMEM((2, history, W, mid), BF16),
            pltpu.VMEM((windows, LAT_CH, 128), BF16),
            pltpu.VMEM((devices, LAT_CH, 128), BF16),
            pltpu.VMEM((history, inner // 2, LAT_CH, 128), BF16),
            pltpu.VMEM((2, history, LAT_CH, 128), BF16),
            pltpu.VMEM((devices, slots), F32),
            pltpu.VMEM((devices, slots), F32),
            pltpu.VMEM((max(devices, windows), slots), F32),
            pltpu.VMEM((devices, lines * LAT_CH, 128), BF16),
            pltpu.VMEM((devices * 128, 128), BF16),
            pltpu.VMEM((2, history + FMAX, mid, stretch + cells), BF16),
            pltpu.VMEM((4, width, 12 * mid), BF16),
            pltpu.VMEM((history, 4, width, cells), F32),
            pltpu.VMEM((mid, stretch), F32),
            pltpu.VMEM((3, mid, 128), F32),
            pltpu.SemaphoreType.DMA((len(inputs),)),
            pltpu.SemaphoreType.DMA((devices,)),
            pltpu.SemaphoreType.DMA((devices,)),
            pltpu.SemaphoreType.DMA((2, history)),
            pltpu.SemaphoreType.DMA((2, history)),
            pltpu.SemaphoreType.DMA((2, history)),
            pltpu.SemaphoreType.DMA((2, history)),
        ],
        compiler_params=pltpu.CompilerParams(
            collective_id=0, has_side_effects=True, vmem_limit_bytes=44 * 1024 * 1024
        ),
    )(*[in_hbm(x) for x in inputs])
    return pl.pallas_call(
        finish_kernel,
        in_specs=[hbm] * 2 + [vmem] * 3,
        out_specs=[hbm] * 3,
        out_shape=[
            jax.ShapeDtypeStruct((FMAX, 2 * inner, width, 2 * W), BF16),
            jax.ShapeDtypeStruct((history, inner, W, mid), BF16),
            jax.ShapeDtypeStruct((history, inner, W * LAT_CH), BF16),
        ],
        scratch_shapes=[
            pltpu.SMEM(assign.shape, assign.dtype),
            pltpu.SMEM(counts.shape, counts.dtype),
            pltpu.VMEM((FMAX, 2 * inner, width, 2 * W), BF16),
            pltpu.VMEM((history, inner, W, mid), BF16),
            pltpu.VMEM((history, inner, W * LAT_CH), BF16),
            pltpu.SemaphoreType.DMA((2,)),
            pltpu.SemaphoreType.DMA((FMAX + 2,)),
        ],
        compiler_params=pltpu.CompilerParams(vmem_limit_bytes=16 * 1024 * 1024),
    )(in_hbm(assign), in_hbm(counts), halves, center, first)


def body(
    latents,
    layout,
    assign,
    counts,
    latent_cache,
    feature_cache,
    first_weight,
    first_bias,
    norm_gain,
    second_weight,
    second_bias,
):
    decoded_frames, feature_next, latent_next = section(
        assign,
        counts,
        latents,
        layout,
        latent_cache,
        feature_cache,
        first_weight,
        first_bias,
        norm_gain,
        jnp.swapaxes(second_weight, 3, 4),
        second_bias,
    )
    return (jnp.swapaxes(decoded_frames, 2, 3), latent_next, feature_next)


def solution(mesh):
    return jax.shard_map(
        body,
        mesh=mesh,
        in_specs=(
            P(None, ("rep", "seq")),
            P("rep", None),
            P("rep"),
            P("rep"),
            P(None, ("rep", "seq"), None),
            P(None, ("rep", "seq"), None, None),
            P(),
            P(),
            P(),
            P(),
            P(),
        ),
        out_specs=(
            P(None, ("rep", "seq"), None, None),
            P(None, ("rep", "seq"), None),
            P(None, ("rep", "seq"), None, None),
        ),
        check_vma=False,
    )
```

time: 33.4 us -> 23.2 us (0.69); the launches traced: 32.8 us -> 23.1 us
  local copies, waits for them, and re-layouts: 5.18 us -> 0 us
  Pallas kernels: 27 us -> 22.4 us
    unnamed x14 -> x0, local copies, waits for them, and re-layouts: 5.18 us -> none
    pallas_call x2, Pallas kernels: 27 us -> 22.4 us  [the longest x1 20.4 us: section(): pl.pallas_call(functools.partial(section_kernel, devices), in_specs=[hbm]...]
where the time goes in v2:
time: 23.2 us; the launch traced here: 23.1 us
  Pallas kernels  22.4 us (97%)
  between operations  0.64 us (3%)
    pallas_call x1, Pallas kernels, section(): pl.pallas_call(functools.partial(section_kernel, devices), in_specs=[hbm]...  20.4 us
    pallas_call x1, Pallas kernels, section(): pl.pallas_call(finish_kernel, in_specs=[hbm] * 2 + [vmem] * 3, out_specs=...  2.03 us

profile of v2, /device:TPU:0, one launch (start us, length us, event | category | flops | bytes accessed | tf_op | source)
XLA Modules:
  0.0 23.1 jit_solution(18018095376808715003)
XLA Ops:
  0.6 20.4 %shard_map.130 = (bf16[3,4,192,256]{3,2,1,0:T(8,128)(2,1)S(1)}, bf16[5,384,640]{2,1,0:T(8,128)(2,1)S(1)}, bf16[16,2560]{1,0:T(8,128)(2,1)S(1)}) custom-call(s32[8]{0:T(128)} %assign_hbm.3, bf16[16,768]{1,0:T(8,128)(2,1)} %latents_hbm.1, s32[16,768]{1,0:T(8,128)} %layout_hbm.1, bf16[2,4,1024]{2,1,0:T(4,128)(2,1)} %latent_cache_hbm.1, ...), custom_call_target="tpu_custom_call" | custom-call | tf_op jit(solution)/shard_map/pallas_call | solution.py:548
  21.0 2.0 %shard_map.131 = (bf16[3,8,192,128]{3,2,1,0:T(8,128)(2,1)}, bf16[2,4,64,384]{3,2,1,0:T(8,128)(2,1)}, bf16[2,4,1024]{2,1,0:T(4,128)(2,1)}) custom-call(s32[8]{0:T(128)} %assign_hbm.3, s32[8]{0:T(128)} %counts_hbm.1, bf16[3,4,192,256]{3,2,1,0:T(8,128)(2,1)S(1)} %get-tuple-element.9.halves, bf16[5,384,640]{2,1,0:T(8,128)(2,1)S(1)} %get-tuple-element.10.center, ...), custom_call_target="tpu_custom_call" | custom-call | tf_op jit(solution)/shard_map/pallas_call | solution.py:586

commit v3 on v2

--- a/solution.py
+++ b/solution.py
@@ -51,6 +51,12 @@
     return jnp.where(mask > 0.0, jnp.concatenate(ranks, axis=1), -1.0)
 
 
+def peer_of(me, i, devices):
+    if devices & (devices - 1):
+        return lax.rem(me + 1 + i, devices)
+    return me ^ (devices - 1 - i)
+
+
 def place_of(device, devices, per_group):
     place = lax.rem(device + per_group // 2, devices)
     return place // per_group, lax.rem(place, per_group)
@@ -59,6 +65,7 @@
 def section_kernel(
     devices,
     assign_hbm,
+    counts_hbm,
     latents_hbm,
     layout_hbm,
     latent_cache_hbm,
@@ -68,10 +75,12 @@
     gain_hbm,
     w2_hbm,
     b2_hbm,
-    halves,
+    frames_out,
     center,
     first,
+    live,
     assign,
+    counts,
     latents,
     layout,
     latent_cache,
@@ -95,6 +104,8 @@
     packed,
     partial,
     pre,
+    turn,
+    mix,
     columns,
     load_sem,
     send_sem,
@@ -117,6 +128,13 @@
     above = lax.rem(me + devices - 1, devices)
     below = lax.rem(me + 1, devices)
 
+    barrier = pltpu.get_barrier_semaphore()
+
+    def greet(i):
+        pl.semaphore_signal(barrier, inc=1, device_id={"seq": peer_of(me, i, devices)})
+
+    trips(devices - 1, greet)
+
     loads = [
         pltpu.make_async_copy(source, target, load_sem.at[i])
         for i, (source, target) in enumerate(
@@ -125,6 +143,7 @@
                 (layout_hbm, layout),
                 (latents_hbm, latents),
                 (latent_cache_hbm, latent_cache),
+                (counts_hbm, counts),
                 (feature_cache_hbm, feature_cache),
                 (w2_hbm, w2),
                 (w1_hbm, w1),
@@ -137,12 +156,6 @@
     for load in loads:
         load.start()
 
-    barrier = pltpu.get_barrier_semaphore()
-
-    def greet(i):
-        pl.semaphore_signal(barrier, inc=1, device_id={"seq": lax.rem(me + 1 + i, devices)})
-
-    trips(devices - 1, greet)
 
     for load in loads[0:4]:
         load.wait()
@@ -206,7 +219,7 @@
         return g * starts + jnp.clip(k - 1, 0, starts - 1)
 
     def copy_to(i):
-        peer = lax.rem(me + 1 + i, devices)
+        peer = peer_of(me, i, devices)
         return pltpu.make_async_remote_copy(
             src_ref=outgoing.at[window_of(peer)],
             dst_ref=incoming.at[me],
@@ -216,8 +229,6 @@
         )
 
     trips(devices - 1, lambda i: copy_to(i).start())
-    for load in loads[4:]:
-        load.wait()
 
     def edge_copies(side):
         peer = (above, below)[side]
@@ -244,6 +255,8 @@
         return copies
 
     has = (position > 0, position < per_group - 1)
+    for load in loads[4:6]:
+        load.wait()
     for side in range(2):
 
         @pl.when(has[side])
@@ -287,45 +300,86 @@
     mid = feature_cache.shape[3]
     width = b2.shape[0]
     cells = inner * W
-    high_rows = inner + 2
-    stretch = high_rows * W
-    col = lane_index((16, stretch)) % W
-    keep = ((col != 0).astype(BF16), None, (col != W - 1).astype(BF16))
-
+    stretch = (inner + 2) * W
     shifted = (feat.at[0], center, feat.at[1])
 
+    def edge_mask(lanes):
+        col = lane_index((16, lanes)) % W
+        return ((col != 0).astype(BF16), None, (col != W - 1).astype(BF16))
+
+    keep = edge_mask(stretch)
+
     def spread(f, value, ch):
-        value = value.astype(BF16)
         for e in range(3):
-            whole = value if e == 1 else pltpu.roll(value, (1, 0, stretch - 1)[e], 1) * keep[e]
-            shifted[e][f, ch : ch + 16, 0:stretch] = whole
-            below = pltpu.roll(value, stretch - W + 1 - e, 1)[:, 0:cells]
-            below = below if e == 1 else below * keep[e][:, 0:cells]
-            shifted[e][f, ch : ch + 16, stretch : stretch + cells] = below
+            moved = value if e == 1 else pltpu.roll(value, (1, 0, stretch - 1)[e], 1) * keep[e]
+            shifted[e][f, ch : ch + 16, 0:stretch] = moved
+
+    def spread_inner(f, value, ch):
+        for e in range(3):
+            moved = value if e == 1 else pltpu.roll(value, (1, 0, cells - 1)[e], 1) * keep[e][:, 0:cells]
+            shifted[e][f, ch : ch + 16, stretch : stretch + cells] = moved
 
     def pack(i):
         at = pl.multiple_of(i * 16, 16)
         for a in range(3):
-            taps = [[w2[a, b, e, pl.ds(at, 16), :].astype(F32) for e in range(3)] for b in range(3)]
+            taps = [[w2[a, b, e, pl.ds(at, 16), :] for e in range(3)] for b in range(3)]
+            add = lambda r, e, q, d: taps[r][e] + taps[q][d]
             for py in range(2):
-                if py == 0:
-                    pair_of_lines = (taps[0], [taps[1][e] + taps[2][e] for e in range(3)])
-                else:
-                    pair_of_lines = ([taps[0][e] + taps[1][e] for e in range(3)], taps[2])
+                edge = 2 * py
+                top, low = (1, 2) if py == 0 else (0, 1)
+                both = [taps[top][e].astype(F32) + taps[low][e].astype(F32) for e in range(3)]
                 for px in range(2):
-                    for iy, taken in enumerate(pair_of_lines):
-                        if px == 0:
-                            pair = (taken[0], taken[1] + taken[2])
-                        else:
-                            pair = (taken[0] + taken[1], taken[2])
-                        for ix, value in enumerate(pair):
-                            start = ((a * 2 + iy) * 2 + ix) * mid
-                            packed[2 * py + px, pl.ds(at, 16), start : start + mid] = value.astype(BF16)
-
+                    one, near, far = (0, 1, 2) if px == 0 else (2, 0, 1)
+                    values = (
+                        (add(top, one, low, one), both[near] + both[far]),
+                        (taps[edge][one], add(edge, near, edge, far)),
+                    )
+                    for side in range(2):
+                        for which in range(2):
+                            ix = which if px == 0 else 1 - which
+                            start = ((side * 3 + a) * 2 + ix) * mid
+                            packed[2 * py + px, pl.ds(at, 16), start : start + mid] = values[side][which].astype(BF16)
+
+    for load in loads[6:]:
+        load.wait()
     lax.fori_loop(0, width // 16, lambda i, c: pack(i) or 0, 0)
     columns[0, 0:mid] = column_of(b1[...].reshape(1, mid), 128)
     columns[1, 0:mid] = column_of(gain[...].reshape(1, mid), 128)
     columns[2, 0:width] = column_of(b2[...].reshape(1, width), 128)
+    pair = 2 * W
+    spot = sublane_index((2 * pair, 2 * pair))
+    goal = spot // pair + 2 * (spot % pair)
+    mix[...] = (lane_index((2 * pair, 2 * pair)) == goal).astype(BF16)
+    request = assign[group]
+    count = jnp.int32(0)
+    for r in range(REQS):
+        count = count + jnp.where(request == r, counts[r], 0)
+    live[...] = jnp.full(live.shape, count, jnp.int32)
+
+    for f in range(history):
+        pre[:, 0:cells] = jnp.transpose(feature_cache[f].reshape(cells, mid).astype(F32))
+        for ch in range(0, mid, 16):
+            spread_inner(f, pre[ch : ch + 16, 0:cells].astype(BF16), ch)
+
+    def convolve(t, phase, pieces):
+        py, px = phase // 2, phase % 2
+        total = None
+        for side, first_a, last_a in pieces:
+            parts = []
+            for a in range(first_a, last_a):
+                for ix in range(2):
+                    begin = stretch if side == 0 else (0 if py == 0 else 2 * W)
+                    parts.append(shifted[px + ix][t + a, :, begin : begin + cells])
+            begin, end = (side * 3 + first_a) * 2 * mid, (side * 3 + last_a) * 2 * mid
+            product = jnp.dot(
+                packed[phase, :, begin:end], jnp.concatenate(parts, axis=0), preferred_element_type=F32
+            )
+            total = product if total is None else total + product
+        return total
+
+    for t in range(history):
+        for phase in range(4):
+            partial[t, phase] = convolve(t, phase, ((0, 0, history - t),))
 
     for side in range(2):
 
@@ -335,35 +389,11 @@
 
         @pl.when(has[side])
         def _arrive():
-            for copy in edge_copies(1 - side):
+            for copy in edge_copies(1 - side)[0::2]:
                 copy.wait_recv()
 
-    for f in range(history):
-        sides = [jnp.where(has[i], halo[i, f], jnp.zeros((), BF16)) for i in range(2)]
-        tall = jnp.concatenate([sides[0], feature_cache[f].reshape(cells, mid), sides[1]], axis=0)
-        pre[...] = jnp.transpose(tall.astype(F32))
-        for ch in range(0, mid, 16):
-            spread(f, pre[ch : ch + 16, :], ch)
-
-    def convolve(t, phase, taken):
-        py, px = phase // 2, phase % 2
-        parts = []
-        for a in taken:
-            for iy in range(2):
-                begin = (0, stretch, 2 * W)[py + iy]
-                for ix in range(2):
-                    parts.append(shifted[px + ix][t + a, :, begin : begin + cells])
-        begin, end = taken[0] * 4 * mid, (taken[-1] + 1) * 4 * mid
-        return jnp.dot(
-            packed[phase, :, begin:end], jnp.concatenate(parts, axis=0), preferred_element_type=F32
-        )
-
-    for t in range(history):
-        for phase in range(4):
-            partial[t, phase] = convolve(t, phase, range(history - t))
-
     def arrive(i):
-        peer = lax.rem(me + 1 + i, devices)
+        peer = peer_of(me, i, devices)
         pltpu.make_async_remote_copy(
             src_ref=outgoing.at[0],
             dst_ref=incoming.at[peer],
@@ -412,39 +442,96 @@
     shifts = [v.astype(BF16) for v in (left, value, right)]
     later = [pltpu.roll(v, total - W, 1).astype(BF16) for v in (left, value, right)]
     row = lane_index((16, stretch)) // W
-    outside = ((row == 0) & jnp.logical_not(has[0])) | ((row == high_rows - 1) & jnp.logical_not(has[1]))
+    outside = (row == 0) & jnp.logical_not(has[0])
+    outside = outside | ((row == inner + 1) & jnp.logical_not(has[1]))
+    inside = jnp.where(outside, 0.0, 0.5)
     bias = jnp.concatenate([columns[2, 0:width]] * (cells // 128), axis=1)
-    for t in range(FMAX):
-        patch = []
-        for a in range(3):
-            for b in range(3):
-                source, begin = (later, 0) if b == 1 else (shifts, b * W)
-                begin += (t + a) * block
-                for e in range(3):
-                    patch.append(source[e][:, begin : begin + stretch])
-        pre[...] = lax.dot_general(
-            w1[...].reshape(27 * LAT_CH, mid),
-            jnp.concatenate(patch, axis=0),
-            (((0,), (0,)), ((), ())),
-            preferred_element_type=F32,
-        )
+    patches = []
+    for a in range(3):
+        for b in range(3):
+            for e in range(3):
+                source = later[e] if b == 1 else shifts[e]
+                begin = a * block + (0 if b == 1 else b * W)
+                patches.append(
+                    jnp.concatenate(
+                        [source[:, begin + t * block : begin + t * block + stretch] for t in range(FMAX)],
+                        axis=1,
+                    )
+                )
+    pre[...] = lax.dot_general(
+        w1[...].reshape(27 * LAT_CH, mid),
+        jnp.concatenate(patches, axis=0),
+        (((0,), (0,)), ((), ())),
+        preferred_element_type=F32,
+    )
+    repeat = lambda x: jnp.concatenate([x] * (stretch // 128), axis=1)
+    biased = lambda t, ch: pre[ch : ch + 16, t * stretch : (t + 1) * stretch] + repeat(
+        columns[0, ch : ch + 16]
+    )
+
+    def norms(t):
         squares = jnp.zeros((16, stretch), F32)
         for ch in range(0, mid, 16):
-            x = pre[ch : ch + 16, :]
-            x = x + jnp.concatenate([columns[0, ch : ch + 16]] * (stretch // 128), axis=1)
-            pre[ch : ch + 16, :] = x
+            x = biased(t, ch)
             squares = squares + x * x
         inverse = lax.rsqrt(jnp.sum(squares, axis=0, keepdims=True) / mid + 1e-06)
-        for ch in range(0, mid, 16):
-            scale = jnp.concatenate([columns[1, ch : ch + 16]] * (stretch // 128), axis=1)
-            x = pre[ch : ch + 16, :] * inverse * scale
-            x = x / (1.0 + jnp.exp(-x))
-            spread(history + t, jnp.where(outside, 0.0, x), ch)
+        return jnp.broadcast_to(inverse, (16, stretch))
+
+    def activate(t, inverse, chs):
+        for ch in chs:
+            x = biased(t, ch) * inverse * repeat(columns[1, ch : ch + 16])
+            y = x * inside
+            y = (y + y * jnp.tanh(0.5 * x)).astype(BF16)
+            spread(history + t, y, ch)
+            own = pltpu.roll(y, stretch - W, 1)[:, 0:cells]
+            spread_inner(history + t, own, ch)
+
+    steps = list(range(0, mid, 16))
+    activate(0, norms(0), steps)
+    alive = live[0:1, :]
+    def emit(t, pieces):
+        shown = jnp.broadcast_to(alive, (width, pair)) > t
+        held = []
         for phase in range(4):
-            result = convolve(t, phase, range(max(history - t, 0), 3))
+            result = convolve(t, phase, pieces)
             if t < history:
                 result = result + partial[t, phase]
-            halves[t, phase] = (result + bias).astype(BF16)
+            held.append((result + bias).astype(BF16))
+            if phase % 2 == 0:
+                continue
+            for i in range(0, inner, 2):
+                both = jnp.concatenate([half[:, i * W : i * W + pair] for half in held], axis=1)
+                mixed = jnp.dot(both, mix[...], preferred_element_type=F32)
+                for j in range(2):
+                    kept = jnp.where(shown, mixed[:, j * pair : (j + 1) * pair], 0.0)
+                    frames_out[t, 2 * (i + j) + phase // 2] = kept.astype(BF16)
+            held = []
+
+    for t in range(FMAX):
+        if t < history:
+            following = norms(t + 1)
+            for phase in range(4):
+                fresh = convolve(t, phase, ((0, history - t, 3), (1, history - t, 3)))
+                partial[t, phase] = partial[t, phase] + fresh
+                activate(t + 1, following, steps[phase * len(steps) // 4 : (phase + 1) * len(steps) // 4])
+        else:
+            emit(t, ((0, 0, 3), (1, 0, 3)))
+    for side in range(2):
+
+        @pl.when(has[side])
+        def _halo():
+            for copy in edge_copies(1 - side)[1::2]:
+                copy.wait_recv()
+
+    for f in range(history):
+        sides = [jnp.where(has[i], halo[i, f], jnp.zeros((), BF16)) for i in range(2)]
+        tall = jnp.concatenate([sides[0], feature_cache[f].reshape(cells, mid), sides[1]], axis=0)
+        turn[:, 0:stretch] = jnp.transpose(tall.astype(F32))
+        for ch in range(0, mid, 16):
+            spread(f, turn[ch : ch + 16, 0:stretch].astype(BF16), ch)
+
+    for t in range(history):
+        emit(t, ((1, 0, history - t),))
 
     trips(devices - 1, lambda i: copy_to(i).wait_send())
     for side in range(2):
@@ -455,34 +542,10 @@
                 copy.wait_send()
 
 
-def finish_kernel(
-    assign_hbm,
-    counts_hbm,
-    halves,
-    center,
-    first,
-    out,
-    carry,
-    latent_next,
-    assign,
-    counts,
-    out_buf,
-    carry_buf,
-    latent_buf,
-    load_sem,
-    sems,
-):
-    loads = [
-        pltpu.make_async_copy(assign_hbm, assign, load_sem.at[0]),
-        pltpu.make_async_copy(counts_hbm, counts, load_sem.at[1]),
-    ]
-    for load in loads:
-        load.start()
-    frames, _, width, cells = halves.shape
+def finish_kernel(frames, center, first, live, out, carry, latent_next, carry_buf, latent_buf, sems):
     history, inner, _, mid = carry.shape
-    devices = lax.axis_size("seq")
-    group, _ = place_of(lax.axis_index("seq"), devices, devices // REQS)
-    pair = 2 * W
+    cells = inner * W
+    block = (inner + 4) * W
     stores = []
 
     def store(source, target):
@@ -490,33 +553,26 @@
         copy.start()
         stores.append(copy)
 
-    spot = sublane_index((2 * pair, 2 * pair))
-    goal = spot // pair + 2 * (spot % pair)
-    mix = (lane_index((2 * pair, 2 * pair)) == goal).astype(BF16)
-    for t in range(frames):
-        if t == 1:
-            for load in loads:
-                load.wait()
-            count = counts[assign[group]]
-        for i in range(0, inner, 2):
-            for py in range(2):
-                both = jnp.concatenate(
-                    [halves[t, 2 * py + px, :, i * W : i * W + pair] for px in range(2)], axis=1
-                )
-                mixed = jnp.dot(both, mix, preferred_element_type=F32).astype(BF16)
-                if t > 0:
-                    mixed = jnp.where(t < count, mixed, jnp.zeros((), BF16))
-                out_buf[t, 2 * i + py] = mixed[:, 0:pair]
-                out_buf[t, 2 * i + 2 + py] = mixed[:, pair : 2 * pair]
-        store(out_buf.at[t], out.at[t])
+    for t in range(FMAX):
+        store(frames.at[t], out.at[t])
+
+    def picked(values):
+        count = jnp.broadcast_to(live[0:1, 0:1], values[0].shape)
+        result = values[0]
+        for n in range(1, FMAX):
+            result = jnp.where(count == n + 1, values[n], result)
+        return result
+
     for i in range(history):
-        turned = jnp.transpose(center[count + i, :, (inner + 2) * W :].astype(F32)).astype(BF16)
-        carry_buf[i] = turned.reshape(inner, W, mid)
+        begin = (inner + 2) * W
+        choice = [center[1 + n + i, :, begin : begin + cells].astype(F32) for n in range(FMAX)]
+        carry_buf[i] = jnp.transpose(picked(choice)).astype(BF16).reshape(inner, W, mid)
     store(carry_buf, carry)
     parts = []
     for i in range(history):
-        start = pl.multiple_of((count + i) * (inner + 4) * W + 2 * W, 128)
-        own = first[:, pl.ds(start, cells)].astype(F32)
+        start = (1 + i) * block + 2 * W
+        choice = [first[:, start + n * block : start + n * block + cells].astype(F32) for n in range(FMAX)]
+        own = picked(choice)
         for r in range(inner):
             parts.append(own[:, r * W : (r + 1) * W])
     stacked = jnp.concatenate(parts, axis=0).astype(BF16)
@@ -544,17 +600,18 @@
     stretch = (inner + 2) * W
     vmem = pl.BlockSpec(memory_space=pltpu.VMEM)
     hbm = pl.BlockSpec(memory_space=pltpu.HBM)
-    inputs = (assign, latents, layout, latent_cache, feature_cache, w1, b1, gain, w2, b2)
-    halves, center, first = pl.pallas_call(
+    inputs = (assign, counts, latents, layout, latent_cache, feature_cache, w1, b1, gain, w2, b2)
+    frames, center, first, live = pl.pallas_call(
         functools.partial(section_kernel, devices),
         in_specs=[hbm] * len(inputs),
-        out_specs=[vmem] * 3,
+        out_specs=[vmem] * 4,
         out_shape=[
-            jax.ShapeDtypeStruct((FMAX, 4, width, cells), BF16),
+            jax.ShapeDtypeStruct((FMAX, 2 * inner, width, 2 * W), BF16),
             jax.ShapeDtypeStruct((history + FMAX, mid, stretch + cells), BF16),
             jax.ShapeDtypeStruct((LAT_CH, (history + FMAX) * (inner + 4) * W), BF16),
+            jax.ShapeDtypeStruct((8, 128), jnp.int32),
         ],
-        scratch_shapes=[(pltpu.SMEM if i < 1 else pltpu.VMEM)(x.shape, x.dtype) for i, x in enumerate(inputs)]
+        scratch_shapes=[(pltpu.SMEM if i < 2 else pltpu.VMEM)(x.shape, x.dtype) for i, x in enumerate(inputs)]
         + [
             pltpu.VMEM((2, history, W, mid), BF16),
             pltpu.VMEM((windows, LAT_CH, 128), BF16),
@@ -569,7 +626,9 @@
             pltpu.VMEM((2, history + FMAX, mid, stretch + cells), BF16),
             pltpu.VMEM((4, width, 12 * mid), BF16),
             pltpu.VMEM((history, 4, width, cells), F32),
+            pltpu.VMEM((mid, FMAX * stretch), F32),
             pltpu.VMEM((mid, stretch), F32),
+            pltpu.VMEM((4 * W, 4 * W), BF16),
             pltpu.VMEM((3, mid, 128), F32),
             pltpu.SemaphoreType.DMA((len(inputs),)),
             pltpu.SemaphoreType.DMA((devices,)),
@@ -585,7 +644,7 @@
     )(*[in_hbm(x) for x in inputs])
     return pl.pallas_call(
         finish_kernel,
-        in_specs=[hbm] * 2 + [vmem] * 3,
+        in_specs=[vmem] * 4,
         out_specs=[hbm] * 3,
         out_shape=[
             jax.ShapeDtypeStruct((FMAX, 2 * inner, width, 2 * W), BF16),
@@ -593,16 +652,12 @@
             jax.ShapeDtypeStruct((history, inner, W * LAT_CH), BF16),
         ],
         scratch_shapes=[
-            pltpu.SMEM(assign.shape, assign.dtype),
-            pltpu.SMEM(counts.shape, counts.dtype),
-            pltpu.VMEM((FMAX, 2 * inner, width, 2 * W), BF16),
             pltpu.VMEM((history, inner, W, mid), BF16),
             pltpu.VMEM((history, inner, W * LAT_CH), BF16),
-            pltpu.SemaphoreType.DMA((2,)),
             pltpu.SemaphoreType.DMA((FMAX + 2,)),
         ],
         compiler_params=pltpu.CompilerParams(vmem_limit_bytes=16 * 1024 * 1024),
-    )(in_hbm(assign), in_hbm(counts), halves, center, first)
+    )(frames, center, first, live)
 
 
 def body(

time: 23.2 us -> 20.9 us (0.901)
  Pallas kernels: 22.4 us -> 20.1 us
    pallas_call x1, Pallas kernels: 20.4 us -> 18.9 us  [section(): pl.pallas_call(functools.partial(section_kernel, devices), in_specs=[hbm]...]
    pallas_call x1, Pallas kernels: 2.03 us -> 1.19 us  [section(): pl.pallas_call(finish_kernel, in_specs=[vmem] * 4, out_specs=[hbm] * 3, o...]
where the time goes in v3:
time: 20.9 us; the launch traced here: 20.8 us
  Pallas kernels  20.1 us (96%)
  between operations  0.64 us (3%)
    pallas_call x1, Pallas kernels, section(): pl.pallas_call(functools.partial(section_kernel, devices), in_specs=[hbm]...  18.9 us
    pallas_call x1, Pallas kernels, section(): pl.pallas_call(finish_kernel, in_specs=[vmem] * 4, out_specs=[hbm] * 3, o...  1.19 us

profile of v3, /device:TPU:0, one launch (start us, length us, event | category | flops | bytes accessed | tf_op | source)
XLA Modules:
  0.0 20.8 jit_solution(17382917949282182488)
XLA Ops:
  0.6 18.9 %shard_map.130 = (bf16[3,8,192,128]{3,2,1,0:T(8,128)(2,1)S(1)}, bf16[5,384,640]{2,1,0:T(8,128)(2,1)S(1)}, bf16[16,2560]{1,0:T(8,128)(2,1)S(1)}, s32[8,128]{1,0:T(8,128)S(1)}) custom-call(s32[8]{0:T(128)} %assign_hbm.1, s32[8]{0:T(128)} %counts_hbm.1, bf16[16,768]{1,0:T(8,128)(2,1)} %latents_hbm.1, s32[16,768]{1,0:T(8,128)} %layout_hbm.1, ...), custom_call_target="tpu_custom_call" | custom-call | tf_op jit(solution)/shard_map/pallas_call | solution.py:604
  19.6 1.2 %shard_map.131 = (bf16[3,8,192,128]{3,2,1,0:T(8,128)(2,1)}, bf16[2,4,64,384]{3,2,1,0:T(8,128)(2,1)}, bf16[2,4,1024]{2,1,0:T(4,128)(2,1)}) custom-call(bf16[3,8,192,128]{3,2,1,0:T(8,128)(2,1)S(1)} %get-tuple-element.10.frames, bf16[5,384,640]{2,1,0:T(8,128)(2,1)S(1)} %get-tuple-element.11.center, bf16[16,2560]{1,0:T(8,128)(2,1)S(1)} %get-tuple-element.12.first, ...), custom_call_target="tpu_custom_call" | custom-call | tf_op jit(solution)/shard_map/pallas_call | solution.py:645

commit v4 on v3

--- a/solution.py
+++ b/solution.py
@@ -105,6 +105,7 @@
     partial,
     pre,
     turn,
+    w1_turned,
     mix,
     columns,
     load_sem,
@@ -130,11 +131,6 @@
 
     barrier = pltpu.get_barrier_semaphore()
 
-    def greet(i):
-        pl.semaphore_signal(barrier, inc=1, device_id={"seq": peer_of(me, i, devices)})
-
-    trips(devices - 1, greet)
-
     loads = [
         pltpu.make_async_copy(source, target, load_sem.at[i])
         for i, (source, target) in enumerate(
@@ -153,7 +149,15 @@
             )
         )
     ]
-    for load in loads:
+    for load in loads[0:4]:
+        load.start()
+
+    def greet(i):
+        pl.semaphore_signal(barrier, inc=1, device_id={"seq": peer_of(me, i, devices)})
+
+    trips(devices - 1, greet)
+
+    for load in loads[4:]:
         load.start()
 
 
@@ -227,8 +231,6 @@
             recv_sem=recv_sem.at[me],
             device_id={"seq": peer},
         )
-
-    trips(devices - 1, lambda i: copy_to(i).start())
 
     def edge_copies(side):
         peer = (above, below)[side]
@@ -255,13 +257,21 @@
         return copies
 
     has = (position > 0, position < per_group - 1)
+    for side in range(2):
+
+        @pl.when(has[side])
+        def _edges():
+            for copy in edge_copies(side)[0::2]:
+                copy.start()
+
+    trips(devices - 1, lambda i: copy_to(i).start())
     for load in loads[4:6]:
         load.wait()
     for side in range(2):
 
         @pl.when(has[side])
         def _start():
-            for copy in edge_copies(side):
+            for copy in edge_copies(side)[1::2]:
                 copy.start()
 
     incoming[me] = outgoing[window_of(me)]
@@ -349,6 +359,7 @@
     pair = 2 * W
     spot = sublane_index((2 * pair, 2 * pair))
     goal = spot // pair + 2 * (spot % pair)
+    w1_turned[...] = jnp.transpose(w1[...].reshape(27 * LAT_CH, mid).astype(F32)).astype(BF16)
     mix[...] = (lane_index((2 * pair, 2 * pair)) == goal).astype(BF16)
     request = assign[group]
     count = jnp.int32(0)
@@ -446,24 +457,18 @@
     outside = outside | ((row == inner + 1) & jnp.logical_not(has[1]))
     inside = jnp.where(outside, 0.0, 0.5)
     bias = jnp.concatenate([columns[2, 0:width]] * (cells // 128), axis=1)
-    patches = []
-    for a in range(3):
-        for b in range(3):
-            for e in range(3):
-                source = later[e] if b == 1 else shifts[e]
-                begin = a * block + (0 if b == 1 else b * W)
-                patches.append(
-                    jnp.concatenate(
-                        [source[:, begin + t * block : begin + t * block + stretch] for t in range(FMAX)],
-                        axis=1,
-                    )
-                )
-    pre[...] = lax.dot_general(
-        w1[...].reshape(27 * LAT_CH, mid),
-        jnp.concatenate(patches, axis=0),
-        (((0,), (0,)), ((), ())),
-        preferred_element_type=F32,
-    )
+    def first_conv(t):
+        patch = []
+        for a in range(3):
+            for b in range(3):
+                for e in range(3):
+                    source = later[e] if b == 1 else shifts[e]
+                    begin = (t + a) * block + (0 if b == 1 else b * W)
+                    patch.append(source[:, begin : begin + stretch])
+        pre[:, t * stretch : (t + 1) * stretch] = jnp.dot(
+            w1_turned[...], jnp.concatenate(patch, axis=0), preferred_element_type=F32
+        )
+
     repeat = lambda x: jnp.concatenate([x] * (stretch // 128), axis=1)
     biased = lambda t, ch: pre[ch : ch + 16, t * stretch : (t + 1) * stretch] + repeat(
         columns[0, ch : ch + 16]
@@ -487,7 +492,11 @@
             spread_inner(history + t, own, ch)
 
     steps = list(range(0, mid, 16))
-    activate(0, norms(0), steps)
+    first_conv(0)
+    scale_0 = norms(0)
+    for t in range(1, FMAX):
+        first_conv(t)
+        activate(0, scale_0, steps[(t - 1) * len(steps) // (FMAX - 1) : t * len(steps) // (FMAX - 1)])
     alive = live[0:1, :]
     def emit(t, pieces):
         shown = jnp.broadcast_to(alive, (width, pair)) > t
@@ -628,6 +637,7 @@
             pltpu.VMEM((history, 4, width, cells), F32),
             pltpu.VMEM((mid, FMAX * stretch), F32),
             pltpu.VMEM((mid, stretch), F32),
+            pltpu.VMEM((mid, 27 * LAT_CH), BF16),
             pltpu.VMEM((4 * W, 4 * W), BF16),
             pltpu.VMEM((3, mid, 128), F32),
             pltpu.SemaphoreType.DMA((len(inputs),)),

time: 20.9 us -> 20.9 us (level)
  no operation moved by 1% of the time
where the time goes in v4:
time: 20.9 us; the launch traced here: 20.7 us
  Pallas kernels  20.1 us (96%)
  between operations  0.64 us (3%)
    pallas_call x1, Pallas kernels, section(): pl.pallas_call(functools.partial(section_kernel, devices), in_specs=[hbm]...  18.9 us
    pallas_call x1, Pallas kernels, section(): pl.pallas_call(finish_kernel, in_specs=[vmem] * 4, out_specs=[hbm] * 3, o...  1.19 us

profile of v4, /device:TPU:0, one launch (start us, length us, event | category | flops | bytes accessed | tf_op | source)
XLA Modules:
  0.0 20.7 jit_solution(5680239022401429898)
XLA Ops:
  0.6 18.9 %shard_map.130 = (bf16[3,8,192,128]{3,2,1,0:T(8,128)(2,1)S(1)}, bf16[5,384,640]{2,1,0:T(8,128)(2,1)S(1)}, bf16[16,2560]{1,0:T(8,128)(2,1)S(1)}, s32[8,128]{1,0:T(8,128)S(1)}) custom-call(s32[8]{0:T(128)} %assign_hbm.1, s32[8]{0:T(128)} %counts_hbm.1, bf16[16,768]{1,0:T(8,128)(2,1)} %latents_hbm.1, s32[16,768]{1,0:T(8,128)} %layout_hbm.1, ...), custom_call_target="tpu_custom_call" | custom-call | tf_op jit(solution)/shard_map/pallas_call | solution.py:613
  19.6 1.2 %shard_map.131 = (bf16[3,8,192,128]{3,2,1,0:T(8,128)(2,1)}, bf16[2,4,64,384]{3,2,1,0:T(8,128)(2,1)}, bf16[2,4,1024]{2,1,0:T(4,128)(2,1)}) custom-call(bf16[3,8,192,128]{3,2,1,0:T(8,128)(2,1)S(1)} %get-tuple-element.10.frames, bf16[5,384,640]{2,1,0:T(8,128)(2,1)S(1)} %get-tuple-element.11.center, bf16[16,2560]{1,0:T(8,128)(2,1)S(1)} %get-tuple-element.12.first, ...), custom_call_target="tpu_custom_call" | custom-call | tf_op jit(solution)/shard_map/pallas_call | solution.py:655
